TPU v7x, 8 devices: a whole 2x2x1 slice. The times are simulated.
8 devices in a mesh: part: 1 (over z), row: 2 (over y), col: 4 (over x, core).
Axes of the slice: x: 2, y: 2, z: 1, core: 2. Of those that a mesh axis runs over, the one named last changes fastest.
Arguments:
- counts: bfloat16 [4096, 32768], P(('part', 'row'), 'col')
- w_init: float32 [4096, 1024], P(('part', 'row'))
- h_init: float32 [1024, 32768], P('part', 'col')
Outputs:
- output 1: float32 [4096, 1024], P(('part', 'row'))
- output 2: float32 [1024, 32768], P('part', 'col')
All inputs are finite; a program needn't handle non-finite values.
Results may differ from a plain program's by a relative error of at most 0.001.
Values are sent between devices in bfloat16 or wider.
A program may use at most 1 GiB of HBM per device.

v0:
```python
import jax
import jax.numpy as jnp
from jax import lax
from jax.sharding import PartitionSpec as P

SWEEPS = 6


def solution(mesh):
    def local_sweeps(count_blk, w_blk, h_blk):
        w_state = w_blk
        h_state = h_blk
        for sweep_idx in range(SWEEPS):
            w_bf = w_state.astype(jnp.bfloat16)
            h_bf = h_state.astype(jnp.bfloat16)
            z_local = jnp.dot(w_bf, h_bf, preferred_element_type=jnp.float32)
            q_local = (count_blk.astype(jnp.float32) / z_local).astype(jnp.bfloat16)
            num_w = lax.dot_general(q_local, h_bf, (((1,), (1,)), ((), ())), preferred_element_type=jnp.float32)
            num_h = lax.dot_general(w_bf, q_local, (((0,), (0,)), ((), ())), preferred_element_type=jnp.float32)
            h_rowsum = jnp.sum(h_state, axis=1)
            w_colsum = jnp.sum(w_state, axis=0)
            num_w = lax.psum(num_w, "col")
            h_rowsum = lax.psum(h_rowsum, "col")
            num_h = lax.psum(num_h, "row")
            w_colsum = lax.psum(w_colsum, "row")
            w_state = w_state * num_w / h_rowsum[None, :]
            h_state = h_state * num_h / w_colsum[:, None]
        return w_state, h_state

    return jax.shard_map(
        local_sweeps,
        mesh=mesh,
        in_specs=(P(("part", "row"), "col"), P(("part", "row"), None), P("part", "col")),
        out_specs=(P(("part", "row"), None), P("part", "col")),
        check_vma=False,
    )
```

profile of v0, /device:TPU:0, one launch (start us, length us, event | category | flops | bytes accessed | tf_op | source)
XLA Modules:
  0.0 6023.1 jit_solution(2715954388558978243)
XLA Ops:
  7.2 50.3 fusion
  101.1 43.5 fusion.21
  200.4 635.4 %all-reduce.20.cloned.1.call-done = f32[1024,8192]{0,1:T(8,128)} async-done(((f32[1024,8192]{0,1:T(8,128)}), f32[1024,8192]{0,1:T(8,128)}) %all-reduce.20.cloned.1.call-update) | async-done | bytes 33554448 | tf_op jit(solution)/shard_map/psum | solution.py:24
  877.3 110.3 %all-reduce.18.cloned.1.call-done = f32[2048,1024]{1,0:T(8,128)} async-done(((f32[2048,1024]{1,0:T(8,128)}), f32[2048,1024]{1,0:T(8,128)}) %all-reduce.18.cloned.1.call-update) | async-done | bytes 8388624 | tf_op jit(solution)/shard_map/psum | solution.py:22
  998.1 46.5 fusion.1
  1088.3 43.3 fusion.36
  1131.7 103.6 %all-reduce.22.cloned.1.call-done = f32[2048,1024]{1,0:T(8,128)} async-done(((f32[2048,1024]{1,0:T(8,128)}), f32[2048,1024]{1,0:T(8,128)}) %all-reduce.22.cloned.1.call-update) | async-done | bytes 8388624 | tf_op jit(solution)/shard_map/psum | solution.py:22
  1251.2 718.6 %all-reduce.24.cloned.1.call-done = f32[1024,8192]{0,1:T(8,128)} async-done(((f32[1024,8192]{0,1:T(8,128)}), f32[1024,8192]{0,1:T(8,128)}) %all-reduce.24.cloned.1.call-update) | async-done | bytes 33554448 | tf_op jit(solution)/shard_map/psum | solution.py:24
  2003.9 46.5 fusion.2
  2050.5 43.3 fusion.33
  2137.3 689.9 %all-reduce.28.cloned.1.call-done = f32[1024,8192]{0,1:T(8,128)} async-done(((f32[1024,8192]{0,1:T(8,128)}), f32[1024,8192]{0,1:T(8,128)}) %all-reduce.28.cloned.1.call-update) | async-done | bytes 33554448 | tf_op jit(solution)/shard_map/psum | solution.py:24
  2868.5 109.8 %all-reduce.26.cloned.1.call-done = f32[2048,1024]{1,0:T(8,128)} async-done(((f32[2048,1024]{1,0:T(8,128)}), f32[2048,1024]{1,0:T(8,128)}) %all-reduce.26.cloned.1.call-update) | async-done | bytes 8388624 | tf_op jit(solution)/shard_map/psum | solution.py:22
  2988.9 46.5 fusion.3
  3079.0 43.3 fusion.30
  3122.4 103.6 %all-reduce.30.cloned.1.call-done = f32[2048,1024]{1,0:T(8,128)} async-done(((f32[2048,1024]{1,0:T(8,128)}), f32[2048,1024]{1,0:T(8,128)}) %all-reduce.30.cloned.1.call-update) | async-done | bytes 8388624 | tf_op jit(solution)/shard_map/psum | solution.py:22
  3241.9 718.7 %all-reduce.32.cloned.1.call-done = f32[1024,8192]{0,1:T(8,128)} async-done(((f32[1024,8192]{0,1:T(8,128)}), f32[1024,8192]{0,1:T(8,128)}) %all-reduce.32.cloned.1.call-update) | async-done | bytes 33554448 | tf_op jit(solution)/shard_map/psum | solution.py:24
  3994.8 46.5 fusion.4
  4041.3 43.3 fusion.27
  4128.1 689.9 %all-reduce.36.cloned.1.call-done = f32[1024,8192]{0,1:T(8,128)} async-done(((f32[1024,8192]{0,1:T(8,128)}), f32[1024,8192]{0,1:T(8,128)}) %all-reduce.36.cloned.1.call-update) | async-done | bytes 33554448 | tf_op jit(solution)/shard_map/psum | solution.py:24
  4859.3 109.8 %all-reduce.34.cloned.1.call-done = f32[2048,1024]{1,0:T(8,128)} async-done(((f32[2048,1024]{1,0:T(8,128)}), f32[2048,1024]{1,0:T(8,128)}) %all-reduce.34.cloned.1.call-update) | async-done | bytes 8388624 | tf_op jit(solution)/shard_map/psum | solution.py:22
  4979.7 46.5 fusion.5
  5069.7 43.3 fusion.24
  5118.6 98.3 %all-reduce.38.cloned.1.call-done = f32[2048,1024]{1,0:T(8,128)} async-done(((f32[2048,1024]{1,0:T(8,128)}), f32[2048,1024]{1,0:T(8,128)}) %all-reduce.38.cloned.1.call-update) | async-done | bytes 8388624 | tf_op jit(solution)/shard_map/psum | solution.py:22
  5229.1 722.1 %all-reduce.40.cloned.1.call-done = f32[1024,8192]{0,1:T(8,128)} async-done(((f32[1024,8192]{0,1:T(8,128)}), f32[1024,8192]{0,1:T(8,128)}) %all-reduce.40.cloned.1.call-update) | async-done | bytes 33554448 | tf_op jit(solution)/shard_map/psum | solution.py:24
  (73 shorter events, 655.6 us)
Async XLA Ops:
  7.2 828.6 %all-reduce.20.cloned.1.call-start = ((), (), s32[]{:S(2)}) async-start(), calls=%async_computation.1 | async-start | bytes 67108864 | tf_op jit(solution)/shard_map/psum | solution.py:24
  100.8 886.7 %all-reduce.18.cloned.1.call-start = ((), (), s32[]{:S(2)}) async-start(), calls=%async_computation | async-start | bytes 16777216 | tf_op jit(solution)/shard_map/psum | solution.py:22
  144.6 1090.7 %all-reduce.22.cloned.1.call-start = ((), (), s32[]{:S(2)}) async-start(), calls=%async_computation.2 | async-start | bytes 16777216 | tf_op jit(solution)/shard_map/psum | solution.py:22
  1087.8 881.9 %all-reduce.24.cloned.1.call-start = ((), (), s32[]{:S(2)}) async-start(), calls=%async_computation.3 | async-start | bytes 67108864 | tf_op jit(solution)/shard_map/psum | solution.py:24
  1131.6 103.7 %copy-start.8 = (f32[1024]{0:T(1024)S(1)}, f32[1024]{0:T(1024)}, u32[]{:S(2)}) copy-start(f32[1024]{0:T(1024)} %get-tuple-element.9) | copy-start | bytes 12292
  1131.6 113.6 %copy-start.3 = (f32[1024]{0:T(1024)S(1)}, f32[1024]{0:T(1024)}, u32[]{:S(2)}) copy-start(f32[1024]{0:T(1024)} %get-tuple-element.30) | copy-start | bytes 12292
  1131.7 1695.5 %all-reduce.28.cloned.1.call-start = ((), (), s32[]{:S(2)}) async-start(), calls=%async_computation.5 | async-start | bytes 67108864 | tf_op jit(solution)/shard_map/psum | solution.py:24
  2093.8 733.4 %copy-start.5 = (f32[1024]{0:T(1024)S(1)}, f32[1024]{0:T(1024)}, u32[]{:S(2)}) copy-start(f32[1024]{0:T(1024)} %get-tuple-element.13) | copy-start | bytes 12292
  2093.8 884.5 %all-reduce.26.cloned.1.call-start = ((), (), s32[]{:S(2)}) async-start(), calls=%async_computation.4 | async-start | bytes 16777216 | tf_op jit(solution)/shard_map/psum | solution.py:22
  2137.2 1088.8 %all-reduce.30.cloned.1.call-start = ((), (), s32[]{:S(2)}) async-start(), calls=%async_computation.6 | async-start | bytes 16777216 | tf_op jit(solution)/shard_map/psum | solution.py:22
  2827.2 33.6 copy-start
  3078.6 882.0 %all-reduce.32.cloned.1.call-start = ((), (), s32[]{:S(2)}) async-start(), calls=%async_computation.7 | async-start | bytes 67108864 | tf_op jit(solution)/shard_map/psum | solution.py:24
  3122.3 103.7 %copy-start.6 = (f32[1024]{0:T(1024)S(1)}, f32[1024]{0:T(1024)}, u32[]{:S(2)}) copy-start(f32[1024]{0:T(1024)} %get-tuple-element.7) | copy-start | bytes 12292
  3122.3 113.7 %copy-start.1 = (f32[1024]{0:T(1024)S(1)}, f32[1024]{0:T(1024)}, u32[]{:S(2)}) copy-start(f32[1024]{0:T(1024)} %get-tuple-element.22) | copy-start | bytes 12292
  3122.4 1695.7 %all-reduce.36.cloned.1.call-start = ((), (), s32[]{:S(2)}) async-start(), calls=%async_computation.9 | async-start | bytes 67108864 | tf_op jit(solution)/shard_map/psum | solution.py:24
  4084.6 733.4 %copy-start.7 = (f32[1024]{0:T(1024)S(1)}, f32[1024]{0:T(1024)}, u32[]{:S(2)}) copy-start(f32[1024]{0:T(1024)} %get-tuple-element.11) | copy-start | bytes 12292
  4084.7 884.5 %all-reduce.34.cloned.1.call-start = ((), (), s32[]{:S(2)}) async-start(), calls=%async_computation.8 | async-start | bytes 16777216 | tf_op jit(solution)/shard_map/psum | solution.py:22
  4128.1 1088.8 %all-reduce.38.cloned.1.call-start = ((), (), s32[]{:S(2)}) async-start(), calls=%async_computation.10 | async-start | bytes 16777216 | tf_op jit(solution)/shard_map/psum | solution.py:22
  4818.0 33.6 copy-start.2
  5069.4 881.7 %all-reduce.40.cloned.1.call-start = ((), (), s32[]{:S(2)}) async-start(), calls=%async_computation.11 | async-start | bytes 67108864 | tf_op jit(solution)/shard_map/psum | solution.py:24
  5113.0 0.7 copy-start.4
  5113.0 103.8 %copy-start.9 = (f32[1024]{0:T(1024)S(1)}, f32[1024]{0:T(1024)}, u32[]{:S(2)}) copy-start(f32[1024]{0:T(1024)} %get-tuple-element.5) | copy-start | bytes 12292
Sparse Core Ops, SparseCore 0:
  100.9 734.7 all-reduce.19
  838.7 148.7 all-reduce.17
  1088.0 147.2 all-reduce.21
  1237.6 732.1 all-reduce.23
  2093.9 733.2 all-reduce.27
  2829.5 148.7 all-reduce.25
  3078.7 147.2 all-reduce.29
  3228.5 732.1 all-reduce.31
  4084.8 733.2 all-reduce.35
  4820.3 148.7 all-reduce.33
  5069.5 147.2 all-reduce.37
  5219.2 731.9 all-reduce.39
where the time goes:
time: 6030 us; the launch traced here: 6020 us
  waiting for transfers between devices  4810 us (80%)
  matrix products  802 us (13%)
  other arithmetic  283 us (5%)
  local copies, waits for them, and re-layouts  65.2 us (1%)
    psum x6, waiting for transfers between devices, local_sweeps(): num_h = lax.psum(num_h, 'row')  4170 us
    psum x6, waiting for transfers between devices, local_sweeps(): num_w = lax.psum(num_w, 'col')  635 us
    dot_general x6, matrix products, local_sweeps(): z_local = jnp.dot(w_bf, h_bf, preferred_element_type=jnp.float32)  283 us
    dot_general x6, matrix products, local_sweeps(): lax.dot_general(w_bf, q_local, (((0,), (0,)), ((), ())), preferred_elemen...  260 us
    dot_general x6, matrix products, local_sweeps(): lax.dot_general(q_local, h_bf, (((1,), (1,)), ((), ())), preferred_elemen...  259 us
    reduce_sum x6, other arithmetic, local_sweeps(): h_rowsum = jnp.sum(h_state, axis=1)  181 us
  transfers between devices with their start and end apart: 12, of which 12 were waited for; matrix products, arithmetic and copies ran while one was open for 7% of the time, Pallas kernels for 0%

commit v1 on v0

v1 whole, which is shorter than its diff:
```python
import functools

import jax
import jax.numpy as jnp
from jax import lax
from jax.experimental import pallas as pl
from jax.experimental.pallas import tpu as pltpu
from jax.sharding import PartitionSpec as P


SWEEPS = 6
BLK = 256
COLBLK = 1024
AXES = ("row", "col")
F32 = jnp.float32
BF16 = jnp.bfloat16


def swap(val, mask):
    return lax.ppermute(val, AXES, [(i, i ^ mask) for i in range(8)])


def swap_by_core(val, mask0, mask1):
    return lax.ppermute(val, AXES, [(i, i ^ (mask1 if i & 1 else mask0)) for i in range(8)])


def dot_nw(q, h_bf):
    return lax.dot_general(q, h_bf, (((1,), (1,)), ((), ())), preferred_element_type=F32)


def dot_nh(w_bf, q):
    return lax.dot_general(w_bf, q, (((0,), (0,)), ((), ())), preferred_element_type=F32)


def quotient(counts, w_bf, h_bf):
    return (counts.astype(F32) / jnp.dot(w_bf, h_bf, preferred_element_type=F32)).astype(BF16)


def pick(arr, idx, axis):
    return lax.dynamic_index_in_dim(arr, idx, axis, keepdims=False)


def assemble_kernel(keys, axis_col, *refs):
    pieces, out_ref, sems = refs[:len(keys)], refs[-2], refs[-1]
    col = lax.axis_index(axis_col)
    core, chip = lax.rem(col, 2), lax.div(col, 2)
    copies = []
    for n, (yrel, xrel, crel) in enumerate(keys):
        core_at = 1 - core if crel else core
        chip_at = 1 - chip if xrel else chip
        start = pl.multiple_of(yrel * 1024 + core_at * 512 + chip_at * BLK, BLK)
        copy = pltpu.make_async_copy(pieces[n], out_ref.at[pl.ds(start, BLK)], sems.at[n])
        copy.start()
        copies.append(copy)
    for copy in copies:
        copy.wait()


def assemble(pieces):
    keys = tuple(pieces)
    val = next(iter(pieces.values()))
    size = len(keys) * BLK
    return pl.pallas_call(
        functools.partial(assemble_kernel, keys, "col"),
        out_shape=jax.ShapeDtypeStruct((size, val.shape[1]), val.dtype),
        in_specs=[pl.BlockSpec(memory_space=pl.ANY)] * len(keys),
        out_specs=pl.BlockSpec(memory_space=pltpu.VMEM),
        scratch_shapes=[pltpu.SemaphoreType.DMA((len(keys),))],
        cost_estimate=pl.CostEstimate(flops=10 ** 9, bytes_accessed=4 * size * val.shape[1], transcendentals=0),
    )(*[pieces[k] for k in keys])


def join_kernel(side_ref, own_ref, oth_ref, out_ref):
    step = pl.program_id(0)

    @pl.when(step < 4)
    def _():
        out_ref[...] = own_ref[...]

    @pl.when(step >= 4)
    def _():
        out_ref[...] = oth_ref[...]


def join_rows(side, c_blk, first_row, c_oth):
    width = c_oth.shape[1]
    base = first_row // BLK
    return pl.pallas_call(
        join_kernel,
        out_shape=jax.ShapeDtypeStruct((2048, width), BF16),
        grid_spec=pltpu.PrefetchScalarGridSpec(
            num_scalar_prefetch=1,
            grid=(8,),
            in_specs=[
                pl.BlockSpec((BLK, width), lambda i, s: (base + jnp.minimum(i, 3), s[0])),
                pl.BlockSpec((BLK, width), lambda i, s: (jnp.maximum(i - 4, 0), 0)),
            ],
            out_specs=pl.BlockSpec((BLK, width), lambda i, s: (i, 0)),
        ),
        cost_estimate=pl.CostEstimate(flops=10 ** 9, bytes_accessed=4 * 2048 * width, transcendentals=0),
    )(jnp.reshape(side, (1,)).astype(jnp.int32), c_blk, c_oth)


def butterfly(vec):
    for mask in (1, 2, 4):
        vec = vec + swap(vec, mask)
    return vec


def solution(mesh):
    def body(c_blk, w_blk, h_blk):
        side = lax.axis_index("row")
        col = lax.axis_index("col")
        core, chip = lax.rem(col, 2), lax.div(col, 2)
        half = h_blk.shape[1] // 2
        mine = side * half
        theirs = (1 - side) * half

        def reduce_set_x(num):
            view = num.reshape(2, 2, 2, BLK, 1024)
            tot = pick(view, core, 1) + swap(pick(view, 1 - core, 1), 1)
            tot = pick(tot, chip, 1) + swap(pick(tot, 1 - chip, 1), 2)
            return tot[0] + swap(tot[1], 4)

        def reduce_set(num):
            view = num.reshape(2, 2, 2, BLK, 1024)
            got = swap(pick(view, 1 - core, 1), 1)
            tot = pick(view, core, 1) + got
            send = jnp.where(core == 0, pick(tot, 1 - chip, 1), tot[1])
            keep = jnp.where(core == 0, pick(tot, chip, 1), tot[0])
            keep = keep + swap_by_core(send, 2, 4)
            away = jnp.where(core == 0, 1, 1 - chip)
            got = swap_by_core(pick(keep, away, 0), 4, 2)
            return pick(keep, 1 - away, 0) + got

        def gather_set(b0):
            pieces = {(0, 0, 0): b0}
            for y, x in ((0, 1), (1, 0), (1, 1)):
                pieces[(y, x, 0)] = swap(b0, 4 * y + 2 * x)
            for y, x in ((0, 0), (0, 1), (1, 0), (1, 1)):
                pieces[(y, x, 1)] = swap(pieces[(y, x, 0)], 1)
            return assemble(pieces)

        def sums(h_part, w_val):
            part = jnp.stack([h_part, jnp.sum(w_val[0], axis=0) + jnp.sum(w_val[1], axis=0)])
            tot = butterfly(part)
            return tot[0], tot[1]

        c_oth = []
        for s in range(2):
            sent = lax.dynamic_slice(c_blk, (s * 1024, theirs), (1024, half))
            c_oth.append(swap(sent, 4))
        h_state = lax.dynamic_slice_in_dim(h_blk, mine, half, 1)
        hb = h_state.astype(BF16)
        hb_theirs = lax.dynamic_slice_in_dim(h_blk, theirs, half, 1).astype(BF16)
        w_own = w_blk.astype(BF16)
        offset = core * 512 + chip * BLK
        w_state = [lax.dynamic_slice_in_dim(w_blk, s * 1024 + offset, BLK, 0) for s in range(2)]
        w_oth = []
        for s in range(2):
            b0 = w_state[s].astype(BF16)
            p10 = swap(b0, 4)
            p11 = swap(b0, 6)
            pieces = {(0, 0, 0): p10, (0, 1, 0): p11, (0, 0, 1): swap(p10, 1), (0, 1, 1): swap(p11, 1)}
            w_oth.append(assemble(pieces))
        h_sum, w_sum = sums(jnp.sum(h_state, axis=1), w_state)
        q_theirs = quotient(lax.dynamic_slice_in_dim(c_blk, theirs, half, 1), w_own, hb_theirs)
        num_t = dot_nw(q_theirs, hb_theirs)
        q_own = quotient(lax.dynamic_slice_in_dim(c_blk, mine, half, 1), w_own, hb)
        num_w = num_t + dot_nw(q_own, hb)
        view = num_w.reshape(2, 2, 2, BLK, 1024)
        tot = pick(view, core, 1) + swap(pick(view, 1 - core, 1), 1)
        num_w = pick(tot, chip, 1) + swap(pick(tot, 1 - chip, 1), 2)
        num_h = dot_nh(w_own, q_own)
        w_state = [lax.optimization_barrier(w_state[s] * num_w[s] / h_sum[None, :]) for s in range(2)]
        w_set = [gather_set(w_state[s].astype(BF16)) for s in range(2)]
        for s in range(2):
            q_oth = quotient(c_oth[s], w_oth[s], hb)
            num_h = num_h + dot_nh(w_oth[s], q_oth)
        counts = [join_rows(side, c_blk, s * 1024, c_oth[s]) for s in range(2)]
        h_state = h_state * num_h / w_sum[:, None]
        hb = h_state.astype(BF16)
        h_part = jnp.sum(h_state, axis=1)

        for _ in range(1, SWEEPS - 1):
            h_sum, w_sum = sums(h_part, w_state)
            q_set, w_next, w_gathered = [], [], []
            for s in range(2):
                q_set.append(quotient(counts[s], w_set[s], hb))
                num_w = reduce_set(dot_nw(q_set[s], hb))
                num_w, h_tot = lax.optimization_barrier((num_w, h_sum))
                w_next.append(lax.optimization_barrier(w_state[s] * num_w / h_tot[None, :]))
                w_gathered.append(gather_set(w_next[s].astype(BF16)))
            num_h = dot_nh(w_set[0], q_set[0]) + dot_nh(w_set[1], q_set[1])
            h_state = h_state * num_h / w_sum[:, None]
            hb = h_state.astype(BF16)
            h_part = jnp.sum(h_state, axis=1)
            w_state = w_next
            w_set = w_gathered

        h_sum, w_sum = sums(h_part, w_state)
        h_out = jnp.zeros(h_blk.shape, F32)
        num_w = [None, None]
        for j in range(half // COLBLK):
            at = slice(j * COLBLK, (j + 1) * COLBLK)
            q_set = [quotient(counts[s][:, at], w_set[s], hb[:, at]) for s in range(2)]
            num_h = dot_nh(w_set[0], q_set[0]) + dot_nh(w_set[1], q_set[1])
            h_fin = h_state[:, at] * num_h / w_sum[:, None]
            h_got = swap(h_fin, 4)
            h_out = lax.dynamic_update_slice_in_dim(h_out, h_fin, mine + j * COLBLK, 1)
            h_out = lax.dynamic_update_slice_in_dim(h_out, h_got, theirs + j * COLBLK, 1)
            for s in range(2):
                part = dot_nw(q_set[s], hb[:, at])
                num_w[s] = part if num_w[s] is None else num_w[s] + part
        w_out = jnp.zeros(w_blk.shape, F32)
        w_fin = []
        for s in range(2):
            tot = reduce_set_x(num_w[s])
            w_fin.append(w_state[s] * tot / h_sum[None, :])
        w_fin = jnp.stack(w_fin)
        w_x = swap(w_fin, 2)
        got = [(0, 0, w_fin), (1, 0, w_x), (0, 1, swap(w_fin, 1)), (1, 1, swap(w_x, 1))]
        for x, c, val in got:
            start = jnp.bitwise_xor(core, c) * 512 + jnp.bitwise_xor(chip, x) * BLK
            for s in range(2):
                w_out = lax.dynamic_update_slice_in_dim(w_out, val[s], s * 1024 + start, 0)
        return w_out, h_out


    return jax.shard_map(
        body,
        mesh=mesh,
        in_specs=(P(("part", "row"), "col"), P(("part", "row"), None), P("part", "col")),
        out_specs=(P(("part", "row"), None), P("part", "col")),
        check_vma=False,
    )
```

time: 6030 us -> 2710 us (0.45)
  waiting for transfers between devices: 4810 us -> 1190 us
  matrix products: 802 us -> 1020 us
  other arithmetic: 283 us -> 81.6 us
  local copies, waits for them, and re-layouts: 65.2 us -> 236 us
  starting transfers between devices: 2.26 us -> 96.2 us
  Pallas kernels: 0 us -> 76.2 us
    psum x12 -> x0, waiting for transfers between devices: 4810 us -> none  [the longest x6 4170 us: local_sweeps(): num_h = lax.psum(num_h, 'row')]
    ppermute x0 -> x137, waiting for transfers between devices: none -> 1190 us  [the longest x121 993 us: swap(): return lax.ppermute(val, AXES, [(i, i ^ mask) for i in range(8)])]
    reduce_sum x12 -> x6, other arithmetic: 237 us -> 12.9 us  [the longest x1 6.74 us: body(): h_sum, w_sum = sums(jnp.sum(h_state, axis=1), w_state)]
    dot_general x18 -> x55, matrix products: 802 us -> 1020 us  [the longest x19 374 us: dot_nh(): lax.dot_general(w_bf, q, (((0,), (0,)), ((), ())), preferred_element_type...]
    ppermute x0 -> x137, starting transfers between devices: none -> 96.2 us  [the longest x121 80.5 us: swap(): return lax.ppermute(val, AXES, [(i, i ^ mask) for i in range(8)])]
    pallas_call x0 -> x14, Pallas kernels: none -> 76.2 us  [the longest x12 47.6 us: assemble(): pl.pallas_call(functools.partial(assemble_kernel, keys, 'col'), out_shape...]
  transfers between devices with their start and end apart: 12 -> 137, of which waited for: 12 -> 39; matrix products, arithmetic and copies ran while one was open for 7% -> 32% of each run, Pallas kernels for 0% -> 3%
where the time goes in v1:
time: 2710 us; the launch traced here: 2700 us
  waiting for transfers between devices  1190 us (44%)
  matrix products  1020 us (38%)
  local copies, waits for them, and re-layouts  236 us (9%)
  starting transfers between devices  96.2 us (4%)
  other arithmetic  81.6 us (3%)
  Pallas kernels  76.2 us (3%)
    ppermute x121, waiting for transfers between devices, swap(): return lax.ppermute(val, AXES, [(i, i ^ mask) for i in range(8)])  993 us
    dot_general x19, matrix products, dot_nh(): lax.dot_general(w_bf, q, (((0,), (0,)), ((), ())), preferred_element_type...  374 us
    dot_general x18, matrix products, quotient(): jnp.dot(w_bf, h_bf, preferred_element_type=F32)  334 us
    dot_general x18, matrix products, dot_nw(): lax.dot_general(q, h_bf, (((1,), (1,)), ((), ())), preferred_element_type...  309 us
    ppermute x16, waiting for transfers between devices, swap_by_core(): lax.ppermute(val, AXES, [(i, i ^ (mask1 if i & 1 else mask0)) for i in ra...  197 us
    unnamed x286, local copies, waits for them, and re-layouts  90.4 us
    ppermute x121, starting transfers between devices, swap(): return lax.ppermute(val, AXES, [(i, i ^ mask) for i in range(8)])  80.5 us
  transfers between devices with their start and end apart: 137, of which 39 were waited for; matrix products, arithmetic and copies ran while one was open for 32% of the time, Pallas kernels for 3%

profile of v1, /device:TPU:0, one launch (start us, length us, event | category | flops | bytes accessed | tf_op | source)
XLA Modules:
  0.0 2699.6 jit_solution(10803860567862026060)
XLA Ops:
  29.0 27.0 %fusion.9.clone.5 = bf16[2048,4096]{1,0:T(8,128)(2,1)} fusion(bf16[2048,8192]{1,0:T(8,128)(2,1)} %own_ref.3, s32[]{:T(128)S(6)} %select_n.211, f32[1024,8192]{1,0:T(8,128)} %param.5, f32[2048,1024]{1,0:T(8,128)} %param.4), kind=kOutput, calls=%fused_computation.19.clone.clone.clone.2 | convolution fusion | flops 17207132160 | bytes 50332672 | tf_op jit(solution)/shard_map/dot_general | solution.py:36
  121.2 27.0 fusion.8
  148.1 37.9 %convolution_add_fusion = f32[2048,1024]{1,0:T(8,128)S(1)} fusion(f32[2048,1024]{1,0:T(8,128)} %fusion.23, bf16[2048,4096]{0,1:T(8,128)(2,1)} %fusion.8, f32[1024,4096]{0,1:T(8,128)} %copy.58), kind=kOutput, calls=%fused_computation.45 | convolution fusion | flops 17186160640 | bytes 50331648 | tf_op jit(solution)/shard_map/dot_general | solution.py:28
  230.2 37.3 %collective-permute-done.3 = f32[2,1024]{1,0:T(2,128)S(1)} collective-permute-done((f32[2,1024]{1,0:T(2,128)S(1)}, f32[2,1024]{1,0:T(2,128)S(1)}, u32[]{:S(2)}, u32[]{:S(2)}) %collective-permute-start.3) | collective-permute-done | bytes 8224 | tf_op jit(solution)/shard_map/ppermute | solution.py:20
  269.3 329.0 %collective-permute-done.4 = f32[2,1024]{1,0:T(2,128)S(1)} collective-permute-done((f32[2,1024]{1,0:T(2,128)S(1)}, f32[2,1024]{1,0:T(2,128)S(1)}, u32[]{:S(2)}, u32[]{:S(2)}) %collective-permute-start.4) | collective-permute-done | bytes 8224 | tf_op jit(solution)/shard_map/ppermute | solution.py:20
  744.5 26.7 fusion.13
  771.3 38.5 %fusion.106 = (f32[1024]{0:T(1024)}, bf16[1024,4096]{0,1:T(8,128)(2,1)}, f32[1024,4096]{0,1:T(8,128)}) fusion(f32[1024]{0:T(1024)S(1)} %bitcast.484, f32[1024,4096]{0,1:T(8,128)} %copy.58, bf16[1024,1024]{1,0:T(8,128)(2,1)S(1)} %copy-done.63, bf16[1024,4096]{1,0:T(8,128)(2,1)} %collective-permute-done.21.oth_ref, f32[1024,4096]{0,1:T(8,128)} %fusion.13, ...), kind=kOutput, calls=%fused_computation.244 | convolution fusion | flops 17221812224 | bytes 85991424 | tf_op jit(solution)/shard_map/dot_general | solution.py:32
  876.8 26.5 fusion
  967.3 28.1 %collective-permute-done.26 = f32[2,1024]{1,0:T(2,128)S(1)} collective-permute-done((f32[2,1024]{1,0:T(2,128)S(1)}, f32[2,1024]{1,0:T(2,128)S(1)}, u32[]{:S(2)}, u32[]{:S(2)}) %collective-permute-start.26) | collective-permute-done | bytes 8224 | tf_op jit(solution)/shard_map/ppermute | solution.py:20
  1008.7 35.6 %collective-permute-done.24 = f32[256,1024]{1,0:T(8,128)S(1)} collective-permute-done((f32[256,1024]{1,0:T(8,128)S(1)}, f32[256,1024]{1,0:T(8,128)S(1)}, u32[]{:S(2)}, u32[]{:S(2)}) %collective-permute-start.24) | collective-permute-done | bytes 1048608 | tf_op jit(solution)/shard_map/ppermute | solution.py:24
  1075.0 32.3 %fusion.105 = (f32[1024]{0:T(1024)}, bf16[1024,4096]{0,1:T(8,128)(2,1)}, f32[1024,4096]{0,1:T(8,128)}) fusion(f32[1024]{0:T(1024)S(1)} %bitcast.489, f32[1024,4096]{0,1:T(8,128)} %get-tuple-element.96, f32[1024,4096]{0,1:T(8,128)} %fusion.130, bf16[2048,1024]{1,0:T(8,128)(2,1)S(1)} %copy-done.46, bf16[2048,4096]{1,0:T(8,128)(2,1)} %fusion), kind=kOutput, calls=%fused_computation.243 | convolution fusion | flops 17200840704 | bytes 79699968 | tf_op jit(solution)/shard_map/dot_general | solution.py:32
  1256.2 31.0 %collective-permute-done.49 = f32[2,1024]{1,0:T(2,128)S(1)} collective-permute-done((f32[2,1024]{1,0:T(2,128)S(1)}, f32[2,1024]{1,0:T(2,128)S(1)}, u32[]{:S(2)}, u32[]{:S(2)}) %collective-permute-start.49) | collective-permute-done | bytes 8224 | tf_op jit(solution)/shard_map/ppermute | solution.py:20
  1296.4 36.0 %collective-permute-done.70 = f32[256,1024]{1,0:T(8,128)S(1)} collective-permute-done((f32[256,1024]{1,0:T(8,128)S(1)}, f32[256,1024]{1,0:T(8,128)S(1)}, u32[]{:S(2)}, u32[]{:S(2)}) %collective-permute-start.70) | collective-permute-done | bytes 1048608 | tf_op jit(solution)/shard_map/ppermute | solution.py:24
  1362.9 32.1 %fusion.104 = (f32[1024]{0:T(1024)}, bf16[1024,4096]{0,1:T(8,128)(2,1)}, f32[1024,4096]{0,1:T(8,128)}) fusion(f32[1024]{0:T(1024)S(1)} %bitcast.490, f32[1024,4096]{0,1:T(8,128)} %get-tuple-element.97, f32[1024,4096]{0,1:T(8,128)} %fusion.133, bf16[2048,1024]{1,0:T(8,128)(2,1)S(1)} %copy-done.47, bf16[2048,4096]{1,0:T(8,128)(2,1)} %fusion.1), kind=kOutput, calls=%fused_computation.242 | convolution fusion | flops 17200840704 | bytes 79699968 | tf_op jit(solution)/shard_map/dot_general | solution.py:32
  1400.2 26.5 fusion.6
  1543.8 31.2 %collective-permute-done.72 = f32[2,1024]{1,0:T(2,128)S(1)} collective-permute-done((f32[2,1024]{1,0:T(2,128)S(1)}, f32[2,1024]{1,0:T(2,128)S(1)}, u32[]{:S(2)}, u32[]{:S(2)}) %collective-permute-start.72) | collective-permute-done | bytes 8224 | tf_op jit(solution)/shard_map/ppermute | solution.py:20
  1584.2 35.7 %collective-permute-done.67 = f32[256,1024]{1,0:T(8,128)S(1)} collective-permute-done((f32[256,1024]{1,0:T(8,128)S(1)}, f32[256,1024]{1,0:T(8,128)S(1)}, u32[]{:S(2)}, u32[]{:S(2)}) %collective-permute-start.67) | collective-permute-done | bytes 1048608 | tf_op jit(solution)/shard_map/ppermute | solution.py:24
  1650.7 32.4 %fusion.103 = (f32[1024]{0:T(1024)}, bf16[1024,4096]{0,1:T(8,128)(2,1)}, f32[1024,4096]{0,1:T(8,128)}) fusion(f32[1024]{0:T(1024)S(1)} %bitcast.491, f32[1024,4096]{0,1:T(8,128)} %get-tuple-element.98, f32[1024,4096]{0,1:T(8,128)} %fusion.136, bf16[2048,1024]{1,0:T(8,128)(2,1)S(1)} %copy-done.49, bf16[2048,4096]{1,0:T(8,128)(2,1)} %fusion.2), kind=kOutput, calls=%fused_computation.241 | convolution fusion | flops 17200840704 | bytes 79699968 | tf_op jit(solution)/shard_map/dot_general | solution.py:32
  1845.9 29.0 %collective-permute-done.115 = f32[2,256,1024]{2,1,0:T(8,128)S(1)} collective-permute-done((f32[2,256,1024]{2,1,0:T(8,128)S(1)}, f32[2,256,1024]{2,1,0:T(8,128)S(1)}, u32[]{:S(2)}, u32[]{:S(2)}) %collective-permute-start.115) | collective-permute-done | bytes 2097184 | tf_op jit(solution)/shard_map/ppermute | solution.py:24
  1877.9 34.2 %fusion.102 = (bf16[1024,4096]{0,1:T(8,128)(2,1)}, f32[1024]{0:T(1024)S(1)}, f32[1024,4096]{0,1:T(8,128)}) fusion(f32[1024]{0:T(1024)S(1)} %bitcast.492, f32[1024,4096]{0,1:T(8,128)} %get-tuple-element.99, f32[1024,4096]{0,1:T(8,128)} %fusion.139, bf16[2048,1024]{1,0:T(8,128)(2,1)} %shard_map.59, bf16[2048,4096]{1,0:T(8,128)(2,1)} %fusion.3), kind=kOutput, calls=%fused_computation.240 | convolution fusion | flops 17200840704 | bytes 79699968 | tf_op jit(solution)/shard_map/dot_general | solution.py:32
  2197.8 26.4 collective-permute-done.112
  2236.7 31.7 %collective-permute-done.128 = f32[2,256,1024]{2,1,0:T(8,128)S(1)} collective-permute-done((f32[2,256,1024]{2,1,0:T(8,128)S(1)}, f32[2,256,1024]{2,1,0:T(8,128)S(1)}, u32[]{:S(2)}, u32[]{:S(2)}) %collective-permute-start.128) | collective-permute-done | bytes 2097184 | tf_op jit(solution)/shard_map/ppermute | solution.py:20
  2270.0 131.8 %collective-permute-done.113 = f32[256,1024]{1,0:T(8,128)S(1)} collective-permute-done((f32[256,1024]{1,0:T(8,128)S(1)}, f32[256,1024]{1,0:T(8,128)S(1)}, u32[]{:S(2)}, u32[]{:S(2)}) %collective-permute-start.113) | collective-permute-done | bytes 1048608 | tf_op jit(solution)/shard_map/ppermute | solution.py:20
  2404.4 198.9 %collective-permute-done.129 = f32[256,1024]{1,0:T(8,128)S(1)} collective-permute-done((f32[256,1024]{1,0:T(8,128)S(1)}, f32[256,1024]{1,0:T(8,128)S(1)}, u32[]{:S(2)}, u32[]{:S(2)}) %collective-permute-start.129) | collective-permute-done | bytes 1048608 | tf_op jit(solution)/shard_map/ppermute | solution.py:20
  (760 shorter events, 1374.3 us)
Async XLA Ops:
  207.0 394.2 %collective-permute-start.1 = (f32[2,256,1024]{2,1,0:T(8,128)}, f32[2,256,1024]{2,1,0:T(8,128)S(1)}, u32[]{:S(2)}, u32[]{:S(2)}) collective-permute-start(f32[2,256,1024]{2,1,0:T(8,128)} %dynamic-slice_bitcast_fusion.10), channel_id=1, source_target_pairs={{0,2},{1,3},{2,0},{3,1},{4,6},{5,7},{6,4},{7,5}} | collective-permute-start | bytes 6291464 | tf_op jit(solution)/shard_map/ppermute | solution.py:20
  211.6 387.0 %collective-permute-start.18 = (bf16[256,1024]{1,0:T(8,128)(2,1)S(1)}, bf16[256,1024]{1,0:T(8,128)(2,1)}, u32[]{:S(2)}, u32[]{:S(2)}) collective-permute-start(bf16[256,1024]{1,0:T(8,128)(2,1)S(1)} %get-tuple-element.60), channel_id=1, source_target_pairs={{0,6},{1,7},{2,4},{3,5},{4,2},{5,3},{6,0},{7,1}} | collective-permute-start | bytes 1572872 | tf_op jit(solution)/shard_map/ppermute | solution.py:20
  224.9 505.4 %collective-permute-start.21 = (bf16[1024,4096]{1,0:T(8,128)(2,1)}, bf16[1024,4096]{1,0:T(8,128)(2,1)}, u32[]{:S(2)}, u32[]{:S(2)}) collective-permute-start(bf16[1024,4096]{1,0:T(8,128)(2,1)} %get-tuple-element.42), channel_id=1, source_target_pairs={{0,4},{1,5},{2,6},{3,7},{4,0},{5,1},{6,2},{7,3}} | collective-permute-start | bytes 25165832 | tf_op jit(solution)/shard_map/ppermute | solution.py:20
  226.7 517.9 %collective-permute-start.5 = (bf16[1024,4096]{1,0:T(8,128)(2,1)}, bf16[1024,4096]{1,0:T(8,128)(2,1)}, u32[]{:S(2)}, u32[]{:S(2)}) collective-permute-start(bf16[1024,4096]{1,0:T(8,128)(2,1)} %get-tuple-element.43), channel_id=1, source_target_pairs={{0,4},{1,5},{2,6},{3,7},{4,0},{5,1},{6,2},{7,3}} | collective-permute-start | bytes 25165832 | tf_op jit(solution)/shard_map/ppermute | solution.py:20
  267.5 330.7 %collective-permute-start.4 = (f32[2,1024]{1,0:T(2,128)S(1)}, f32[2,1024]{1,0:T(2,128)S(1)}, u32[]{:S(2)}, u32[]{:S(2)}) collective-permute-start(f32[2,1024]{1,0:T(2,128)S(1)} %fusion.236), channel_id=1, source_target_pairs={{0,4},{1,5},{2,6},{3,7},{4,0},{5,1},{6,2},{7,3}} | collective-permute-start | bytes 24584 | tf_op jit(solution)/shard_map/ppermute | solution.py:20
  862.4 68.0 %collective-permute-start.45 = (f32[2,2,256,1024]{3,2,1,0:T(8,128)}, f32[2,2,256,1024]{3,2,1,0:T(8,128)}, u32[]{:S(2)}, u32[]{:S(2)}) collective-permute-start(f32[2,2,256,1024]{3,2,1,0:T(8,128)} %dynamic-slice_bitcast_fusion.5), channel_id=1, source_target_pairs={{0,1},{1,0},{2,3},{3,2},{4,5},{5,4},{6,7},{7,6}} | collective-permute-start | bytes 12582920 | tf_op jit(solution)/shard_map/ppermute | solution.py:20
  1005.8 66.4 %collective-permute-start.60 = (bf16[256,1024]{1,0:T(8,128)(2,1)S(1)}, bf16[256,1024]{1,0:T(8,128)(2,1)S(1)}, u32[]{:S(2)}, u32[]{:S(2)}) collective-permute-start(bf16[256,1024]{1,0:T(8,128)(2,1)S(1)} %get-tuple-element.76.refs_0_), channel_id=1, source_target_pairs={{0,6},{1,7},{2,4},{3,5},{4,2},{5,3},{6,0},{7,1}} | collective-permute-start | bytes 1572872 | tf_op jit(solution)/shard_map/ppermute | solution.py:20
  1007.6 66.1 %collective-permute-start.59 = (bf16[256,1024]{1,0:T(8,128)(2,1)S(1)}, bf16[256,1024]{1,0:T(8,128)(2,1)S(1)}, u32[]{:S(2)}, u32[]{:S(2)}) collective-permute-start(bf16[256,1024]{1,0:T(8,128)(2,1)S(1)} %get-tuple-element.76.refs_0_), channel_id=1, source_target_pairs={{0,4},{1,5},{2,6},{3,7},{4,0},{5,1},{6,2},{7,3}} | collective-permute-start | bytes 1572872 | tf_op jit(solution)/shard_map/ppermute | solution.py:20
  1229.8 61.0 %collective-permute-start.69 = (f32[2,256,1024]{2,1,0:T(8,128)S(1)}, f32[2,256,1024]{2,1,0:T(8,128)S(1)}, u32[]{:S(2)}, u32[]{:S(2)}) collective-permute-start(f32[2,256,1024]{2,1,0:T(8,128)S(1)} %fusion.33), channel_id=1, source_target_pairs={{0,2},{1,5},{2,0},{3,7},{4,6},{5,1},{6,4},{7,3}} | collective-permute-start | bytes 6291464 | tf_op jit(solution)/shard_map/ppermute | solution.py:24
  1293.8 66.8 %collective-permute-start.53 = (bf16[256,1024]{1,0:T(8,128)(2,1)S(1)}, bf16[256,1024]{1,0:T(8,128)(2,1)S(1)}, u32[]{:S(2)}, u32[]{:S(2)}) collective-permute-start(bf16[256,1024]{1,0:T(8,128)(2,1)S(1)} %get-tuple-element.75.refs_0_), channel_id=1, source_target_pairs={{0,6},{1,7},{2,4},{3,5},{4,2},{5,3},{6,0},{7,1}} | collective-permute-start | bytes 1572872 | tf_op jit(solution)/shard_map/ppermute | solution.py:20
  1295.3 66.2 %collective-permute-start.52 = (bf16[256,1024]{1,0:T(8,128)(2,1)S(1)}, bf16[256,1024]{1,0:T(8,128)(2,1)S(1)}, u32[]{:S(2)}, u32[]{:S(2)}) collective-permute-start(bf16[256,1024]{1,0:T(8,128)(2,1)S(1)} %get-tuple-element.75.refs_0_), channel_id=1, source_target_pairs={{0,4},{1,5},{2,6},{3,7},{4,0},{5,1},{6,2},{7,3}} | collective-permute-start | bytes 1572872 | tf_op jit(solution)/shard_map/ppermute | solution.py:20
  1581.7 66.3 %collective-permute-start.106 = (bf16[256,1024]{1,0:T(8,128)(2,1)S(1)}, bf16[256,1024]{1,0:T(8,128)(2,1)S(1)}, u32[]{:S(2)}, u32[]{:S(2)}) collective-permute-start(bf16[256,1024]{1,0:T(8,128)(2,1)S(1)} %get-tuple-element.68.refs_0_), channel_id=1, source_target_pairs={{0,6},{1,7},{2,4},{3,5},{4,2},{5,3},{6,0},{7,1}} | collective-permute-start | bytes 1572872 | tf_op jit(solution)/shard_map/ppermute | solution.py:20
  1583.2 66.1 %collective-permute-start.105 = (bf16[256,1024]{1,0:T(8,128)(2,1)S(1)}, bf16[256,1024]{1,0:T(8,128)(2,1)S(1)}, u32[]{:S(2)}, u32[]{:S(2)}) collective-permute-start(bf16[256,1024]{1,0:T(8,128)(2,1)S(1)} %get-tuple-element.68.refs_0_), channel_id=1, source_target_pairs={{0,4},{1,5},{2,6},{3,7},{4,0},{5,1},{6,2},{7,3}} | collective-permute-start | bytes 1572872 | tf_op jit(solution)/shard_map/ppermute | solution.py:20
  1741.0 69.2 %collective-permute-start.88 = (f32[2,2,256,1024]{3,2,1,0:T(8,128)}, f32[2,2,256,1024]{3,2,1,0:T(8,128)}, u32[]{:S(2)}, u32[]{:S(2)}) collective-permute-start(f32[2,2,256,1024]{3,2,1,0:T(8,128)} %dynamic-slice_bitcast_fusion.2), channel_id=1, source_target_pairs={{0,1},{1,0},{2,3},{3,2},{4,5},{5,4},{6,7},{7,6}} | collective-permute-start | bytes 12582920 | tf_op jit(solution)/shard_map/ppermute | solution.py:20
  1844.6 67.5 %collective-permute-start.90 = (f32[256,1024]{1,0:T(8,128)S(1)}, f32[256,1024]{1,0:T(8,128)}, u32[]{:S(2)}, u32[]{:S(2)}) collective-permute-start(f32[256,1024]{1,0:T(8,128)S(1)} %dynamic-slice_bitcast_fusion.13), channel_id=1, source_target_pairs={{0,4},{1,3},{2,6},{3,1},{4,0},{5,7},{6,2},{7,5}} | collective-permute-start | bytes 3145736 | tf_op jit(solution)/shard_map/ppermute | solution.py:24
  2187.5 80.9 %collective-permute-start.128 = (f32[2,256,1024]{2,1,0:T(8,128)S(1)}, f32[2,256,1024]{2,1,0:T(8,128)S(1)}, u32[]{:S(2)}, u32[]{:S(2)}) collective-permute-start(f32[2,256,1024]{2,1,0:T(8,128)S(1)} %dynamic-slice_bitcast_fusion.8), channel_id=1, source_target_pairs={{0,2},{1,3},{2,0},{3,1},{4,6},{5,7},{6,4},{7,5}} | collective-permute-start | bytes 6291464 | tf_op jit(solution)/shard_map/ppermute | solution.py:20
  2195.7 418.9 %collective-permute-start.136 = (f32[1024,1024]{0,1:T(8,128)}, f32[1024,1024]{0,1:T(8,128)}, u32[]{:S(2)}, u32[]{:S(2)}) collective-permute-start(f32[1024,1024]{0,1:T(8,128)} %fusion.19), channel_id=1, source_target_pairs={{0,4},{1,5},{2,6},{3,7},{4,0},{5,1},{6,2},{7,3}} | collective-permute-start | bytes 12582920 | tf_op jit(solution)/shard_map/ppermute | solution.py:20
  2196.7 453.4 %collective-permute-start.135 = (f32[1024,1024]{0,1:T(8,128)}, f32[1024,1024]{0,1:T(8,128)}, u32[]{:S(2)}, u32[]{:S(2)}) collective-permute-start(f32[1024,1024]{0,1:T(8,128)} %fusion.20), channel_id=1, source_target_pairs={{0,4},{1,5},{2,6},{3,7},{4,0},{5,1},{6,2},{7,3}} | collective-permute-start | bytes 12582920 | tf_op jit(solution)/shard_map/ppermute | solution.py:20
  2224.8 177.0 %collective-permute-start.113 = (f32[256,1024]{1,0:T(8,128)S(1)}, f32[256,1024]{1,0:T(8,128)S(1)}, u32[]{:S(2)}, u32[]{:S(2)}) collective-permute-start(f32[256,1024]{1,0:T(8,128)S(1)} %slice_bitcast_fusion.24), channel_id=1, source_target_pairs={{0,4},{1,5},{2,6},{3,7},{4,0},{5,1},{6,2},{7,3}} | collective-permute-start | bytes 3145736 | tf_op jit(solution)/shard_map/ppermute | solution.py:20
  2235.6 419.8 %collective-permute-start.134 = (f32[1024,1024]{0,1:T(8,128)}, f32[1024,1024]{0,1:T(8,128)}, u32[]{:S(2)}, u32[]{:S(2)}) collective-permute-start(f32[1024,1024]{0,1:T(8,128)} %fusion.21), channel_id=1, source_target_pairs={{0,4},{1,5},{2,6},{3,7},{4,0},{5,1},{6,2},{7,3}} | collective-permute-start | bytes 12582920 | tf_op jit(solution)/shard_map/ppermute | solution.py:20
  2268.4 392.4 %collective-permute-start.133 = (f32[1024,1024]{0,1:T(8,128)}, f32[1024,1024]{0,1:T(8,128)}, u32[]{:S(2)}, u32[]{:S(2)}) collective-permute-start(f32[1024,1024]{0,1:T(8,128)} %fusion.22), channel_id=1, source_target_pairs={{0,4},{1,5},{2,6},{3,7},{4,0},{5,1},{6,2},{7,3}} | collective-permute-start | bytes 12582920 | tf_op jit(solution)/shard_map/ppermute | solution.py:20
  2401.7 201.5 %collective-permute-start.129 = (f32[256,1024]{1,0:T(8,128)S(1)}, f32[256,1024]{1,0:T(8,128)S(1)}, u32[]{:S(2)}, u32[]{:S(2)}) collective-permute-start(f32[256,1024]{1,0:T(8,128)S(1)} %slice_bitcast_fusion.22), channel_id=1, source_target_pairs={{0,4},{1,5},{2,6},{3,7},{4,0},{5,1},{6,2},{7,3}} | collective-permute-start | bytes 3145736 | tf_op jit(solution)/shard_map/ppermute | solution.py:20
  2608.5 65.1 %collective-permute-start.130 = (f32[2,256,1024]{2,1,0:T(8,128)}, f32[2,256,1024]{2,1,0:T(8,128)S(1)}, u32[]{:S(2)}, u32[]{:S(2)}) collective-permute-start(f32[2,256,1024]{2,1,0:T(8,128)} %pad_maximum_fusion), channel_id=1, source_target_pairs={{0,2},{1,3},{2,0},{3,1},{4,6},{5,7},{6,4},{7,5}} | collective-permute-start | bytes 6291464 | tf_op jit(solution)/shard_map/ppermute | solution.py:20
  2614.6 78.1 %collective-permute-start.131 = (f32[2,256,1024]{2,1,0:T(8,128)}, f32[2,256,1024]{2,1,0:T(8,128)}, u32[]{:S(2)}, u32[]{:S(2)}) collective-permute-start(f32[2,256,1024]{2,1,0:T(8,128)} %pad_maximum_fusion), channel_id=1, source_target_pairs={{0,1},{1,0},{2,3},{3,2},{4,5},{5,4},{6,7},{7,6}} | collective-permute-start | bytes 6291464 | tf_op jit(solution)/shard_map/ppermute | solution.py:20
  (255 other events, 5828.3 us)

commit v2 on v1

--- a/solution.py
+++ b/solution.py
@@ -10,7 +10,7 @@
 
 SWEEPS = 6
 BLK = 256
-COLBLK = 1024
+CUTS = (0, 512, 1536, 2560, 3584, 4096)
 AXES = ("row", "col")
 F32 = jnp.float32
 BF16 = jnp.bfloat16
@@ -70,20 +70,24 @@
     )(*[pieces[k] for k in keys])
 
 
-def join_kernel(side_ref, own_ref, oth_ref, out_ref):
+def join_kernel(side_ref, own_ref, oth0_ref, oth1_ref, out_ref):
     step = pl.program_id(0)
 
     @pl.when(step < 4)
     def _():
         out_ref[...] = own_ref[...]
 
-    @pl.when(step >= 4)
+    @pl.when((step >= 4) & (step < 6))
     def _():
-        out_ref[...] = oth_ref[...]
+        out_ref[...] = oth0_ref[...]
+
+    @pl.when(step >= 6)
+    def _():
+        out_ref[...] = oth1_ref[...]
 
 
 def join_rows(side, c_blk, first_row, c_oth):
-    width = c_oth.shape[1]
+    width = c_oth[0].shape[1]
     base = first_row // BLK
     return pl.pallas_call(
         join_kernel,
@@ -93,12 +97,13 @@
             grid=(8,),
             in_specs=[
                 pl.BlockSpec((BLK, width), lambda i, s: (base + jnp.minimum(i, 3), s[0])),
-                pl.BlockSpec((BLK, width), lambda i, s: (jnp.maximum(i - 4, 0), 0)),
+                pl.BlockSpec((BLK, width), lambda i, s: (jnp.clip(i - 4, 0, 1), 0)),
+                pl.BlockSpec((BLK, width), lambda i, s: (jnp.clip(i - 6, 0, 1), 0)),
             ],
             out_specs=pl.BlockSpec((BLK, width), lambda i, s: (i, 0)),
         ),
         cost_estimate=pl.CostEstimate(flops=10 ** 9, bytes_accessed=4 * 2048 * width, transcendentals=0),
-    )(jnp.reshape(side, (1,)).astype(jnp.int32), c_blk, c_oth)
+    )(jnp.reshape(side, (1,)).astype(jnp.int32), c_blk, *c_oth)
 
 
 def butterfly(vec):
@@ -133,23 +138,27 @@
             got = swap_by_core(pick(keep, away, 0), 4, 2)
             return pick(keep, 1 - away, 0) + got
 
-        def gather_set(b0):
+        def gather_set(b0, relay=False):
             pieces = {(0, 0, 0): b0}
             for y, x in ((0, 1), (1, 0), (1, 1)):
-                pieces[(y, x, 0)] = swap(b0, 4 * y + 2 * x)
+                if relay and y and x:
+                    pieces[(y, x, 0)] = swap(pieces[(1, 0, 0)], 2)
+                else:
+                    pieces[(y, x, 0)] = swap(b0, 4 * y + 2 * x)
             for y, x in ((0, 0), (0, 1), (1, 0), (1, 1)):
                 pieces[(y, x, 1)] = swap(pieces[(y, x, 0)], 1)
             return assemble(pieces)
 
         def sums(h_part, w_val):
+            w_val = lax.optimization_barrier(tuple(w_val))
             part = jnp.stack([h_part, jnp.sum(w_val[0], axis=0) + jnp.sum(w_val[1], axis=0)])
             tot = butterfly(part)
             return tot[0], tot[1]
 
         c_oth = []
-        for s in range(2):
-            sent = lax.dynamic_slice(c_blk, (s * 1024, theirs), (1024, half))
-            c_oth.append(swap(sent, 4))
+        for p in range(4):
+            sent = lax.dynamic_slice(c_blk, (p * 512, theirs), (512, half))
+            c_oth.append(swap(lax.optimization_barrier(sent), 4))
         h_state = lax.dynamic_slice_in_dim(h_blk, mine, half, 1)
         hb = h_state.astype(BF16)
         hb_theirs = lax.dynamic_slice_in_dim(h_blk, theirs, half, 1).astype(BF16)
@@ -160,10 +169,15 @@
         for s in range(2):
             b0 = w_state[s].astype(BF16)
             p10 = swap(b0, 4)
-            p11 = swap(b0, 6)
+            p11 = swap(p10, 2)
             pieces = {(0, 0, 0): p10, (0, 1, 0): p11, (0, 0, 1): swap(p10, 1), (0, 1, 1): swap(p11, 1)}
             w_oth.append(assemble(pieces))
-        h_sum, w_sum = sums(jnp.sum(h_state, axis=1), w_state)
+        w_sum = jnp.sum(w_blk, axis=0)[None, :]
+        w_sum = (w_sum + swap(w_sum, 4))[0]
+        h_sum = jnp.sum(h_blk, axis=1)[None, :]
+        for mask in (1, 2):
+            h_sum = h_sum + swap(h_sum, mask)
+        h_sum = h_sum[0]
         q_theirs = quotient(lax.dynamic_slice_in_dim(c_blk, theirs, half, 1), w_own, hb_theirs)
         num_t = dot_nw(q_theirs, hb_theirs)
         q_own = quotient(lax.dynamic_slice_in_dim(c_blk, mine, half, 1), w_own, hb)
@@ -173,11 +187,12 @@
         num_w = pick(tot, chip, 1) + swap(pick(tot, 1 - chip, 1), 2)
         num_h = dot_nh(w_own, q_own)
         w_state = [lax.optimization_barrier(w_state[s] * num_w[s] / h_sum[None, :]) for s in range(2)]
-        w_set = [gather_set(w_state[s].astype(BF16)) for s in range(2)]
-        for s in range(2):
-            q_oth = quotient(c_oth[s], w_oth[s], hb)
-            num_h = num_h + dot_nh(w_oth[s], q_oth)
-        counts = [join_rows(side, c_blk, s * 1024, c_oth[s]) for s in range(2)]
+        w_set = [gather_set(w_state[s].astype(BF16), relay=True) for s in range(2)]
+        for p in range(4):
+            w_part = w_oth[p // 2][(p % 2) * 512:(p % 2) * 512 + 512]
+            q_oth = quotient(c_oth[p], w_part, hb)
+            num_h = num_h + dot_nh(w_part, q_oth)
+        counts = [join_rows(side, c_blk, s * 1024, c_oth[2 * s:2 * s + 2]) for s in range(2)]
         h_state = h_state * num_h / w_sum[:, None]
         hb = h_state.astype(BF16)
         h_part = jnp.sum(h_state, axis=1)
@@ -201,14 +216,15 @@
         h_sum, w_sum = sums(h_part, w_state)
         h_out = jnp.zeros(h_blk.shape, F32)
         num_w = [None, None]
-        for j in range(half // COLBLK):
-            at = slice(j * COLBLK, (j + 1) * COLBLK)
+        for lo, hi in zip(CUTS[:-1], CUTS[1:]):
+            at = slice(lo, hi)
             q_set = [quotient(counts[s][:, at], w_set[s], hb[:, at]) for s in range(2)]
             num_h = dot_nh(w_set[0], q_set[0]) + dot_nh(w_set[1], q_set[1])
             h_fin = h_state[:, at] * num_h / w_sum[:, None]
             h_got = swap(h_fin, 4)
-            h_out = lax.dynamic_update_slice_in_dim(h_out, h_fin, mine + j * COLBLK, 1)
-            h_out = lax.dynamic_update_slice_in_dim(h_out, h_got, theirs + j * COLBLK, 1)
+            h_out = lax.dynamic_update_slice_in_dim(h_out, h_fin, mine + lo, 1)
+            if hi < half:
+                h_out = lax.dynamic_update_slice_in_dim(h_out, h_got, theirs + lo, 1)
             for s in range(2):
                 part = dot_nw(q_set[s], hb[:, at])
                 num_w[s] = part if num_w[s] is None else num_w[s] + part
@@ -224,7 +240,8 @@
             start = jnp.bitwise_xor(core, c) * 512 + jnp.bitwise_xor(chip, x) * BLK
             for s in range(2):
                 w_out = lax.dynamic_update_slice_in_dim(w_out, val[s], s * 1024 + start, 0)
-        return w_out, h_out
+        w_out, h_got = lax.optimization_barrier((w_out, h_got))
+        return w_out, lax.dynamic_update_slice_in_dim(h_out, h_got, theirs + CUTS[-2], 1)
 
 
     return jax.shard_map(

time: 2710 us -> 2430 us (0.90)
  waiting for transfers between devices: 1190 us -> 801 us
  matrix products: 1020 us -> 1060 us
  other arithmetic: 81.6 us -> 119 us
  local copies, waits for them, and re-layouts: 236 us -> 269 us
    ppermute x121 -> x124, waiting for transfers between devices: 993 us -> 627 us  [swap(): return lax.ppermute(val, AXES, [(i, i ^ mask) for i in range(8)])]
    dot_general x19 -> x23, matrix products: 374 us -> 398 us  [dot_nh(): lax.dot_general(w_bf, q, (((0,), (0,)), ((), ())), preferred_element_type...]
    dot_general x18 -> x21, matrix products: 334 us -> 349 us  [quotient(): jnp.dot(w_bf, h_bf, preferred_element_type=F32)]
    unnamed x286 -> x278, local copies, waits for them, and re-layouts: 90.4 us -> 97.7 us
    dot_general x18 -> x20, matrix products: 309 us -> 315 us  [dot_nw(): lax.dot_general(q, h_bf, (((1,), (1,)), ((), ())), preferred_element_type...]
    ppermute x121 -> x124, starting transfers between devices: 80.5 us -> 79.2 us  [swap(): return lax.ppermute(val, AXES, [(i, i ^ mask) for i in range(8)])]
  transfers between devices with their start and end apart: 137 -> 140, of which waited for: 39 -> 34; matrix products, arithmetic and copies ran while one was open for 32% -> 53% of each run, Pallas kernels for 3% -> 3%
where the time goes in v2:
time: 2430 us; the launch traced here: 2420 us
  matrix products  1060 us (44%)
  waiting for transfers between devices  801 us (33%)
  local copies, waits for them, and re-layouts  269 us (11%)
  other arithmetic  119 us (5%)
  starting transfers between devices  91.8 us (4%)
  Pallas kernels  76.9 us (3%)
    ppermute x124, waiting for transfers between devices, swap(): return lax.ppermute(val, AXES, [(i, i ^ mask) for i in range(8)])  627 us
    dot_general x23, matrix products, dot_nh(): lax.dot_general(w_bf, q, (((0,), (0,)), ((), ())), preferred_element_type...  398 us
    dot_general x21, matrix products, quotient(): jnp.dot(w_bf, h_bf, preferred_element_type=F32)  349 us
    dot_general x20, matrix products, dot_nw(): lax.dot_general(q, h_bf, (((1,), (1,)), ((), ())), preferred_element_type...  315 us
    ppermute x16, waiting for transfers between devices, swap_by_core(): lax.ppermute(val, AXES, [(i, i ^ (mask1 if i & 1 else mask0)) for i in ra...  174 us
    unnamed x278, local copies, waits for them, and re-layouts  97.7 us
    ppermute x124, starting transfers between devices, swap(): return lax.ppermute(val, AXES, [(i, i ^ mask) for i in range(8)])  79.2 us
  transfers between devices with their start and end apart: 140, of which 34 were waited for; matrix products, arithmetic and copies ran while one was open for 53% of the time, Pallas kernels for 3%

profile of v2, /device:TPU:0, one launch (start us, length us, event | category | flops | bytes accessed | tf_op | source)
XLA Modules:
  0.0 2422.8 jit_solution(7783533436440629541)
XLA Ops:
  53.6 27.0 %fusion.9.clone.5 = bf16[2048,4096]{1,0:T(8,128)(2,1)} fusion(bf16[2048,8192]{1,0:T(8,128)(2,1)} %own_ref.3, s32[]{:T(128)S(6)} %select_n.219, f32[1024,8192]{1,0:T(8,128)} %param.5, f32[2048,1024]{1,0:T(8,128)} %param.4), kind=kOutput, calls=%fused_computation.19.clone.clone.clone.2 | convolution fusion | flops 17207132160 | bytes 50332672 | tf_op jit(solution)/shard_map/dot_general | solution.py:36
  154.9 27.1 %fusion.8 = bf16[2048,4096]{0,1:T(8,128)(2,1)} fusion(bf16[2048,4096]{0,1:T(8,128)(2,1)} %copy.67, bf16[1024,4096]{0,1:T(8,128)(2,1)} %convert_element_type.197, f32[2048,1024]{1,0:T(8,128)} %param.4), kind=kOutput, calls=%fused_computation.17 | convolution fusion | flops 17207132160 | bytes 50331648 | tf_op jit(solution)/shard_map/dot_general | solution.py:36
  277.2 48.7 %collective-permute-done.5.oth1_ref = bf16[512,4096]{1,0:T(8,128)(2,1)} collective-permute-done((bf16[512,4096]{1,0:T(8,128)(2,1)}, bf16[512,4096]{1,0:T(8,128)(2,1)}, u32[]{:S(2)}, u32[]{:S(2)}) %collective-permute-start.5) | collective-permute-done | bytes 4194336 | tf_op jit(solution)/shard_map/ppermute | solution.py:20
  343.7 72.0 %collective-permute-done.4.oth0_ref = bf16[512,4096]{1,0:T(8,128)(2,1)} collective-permute-done((bf16[512,4096]{1,0:T(8,128)(2,1)}, bf16[512,4096]{1,0:T(8,128)(2,1)}, u32[]{:S(2)}, u32[]{:S(2)}) %collective-permute-start.4) | collective-permute-done | bytes 4194336 | tf_op jit(solution)/shard_map/ppermute | solution.py:20
  440.0 65.6 %collective-permute-done.21.oth0_ref = bf16[512,4096]{1,0:T(8,128)(2,1)} collective-permute-done((bf16[512,4096]{1,0:T(8,128)(2,1)}, bf16[512,4096]{1,0:T(8,128)(2,1)}, u32[]{:S(2)}, u32[]{:S(2)}) %collective-permute-start.21) | collective-permute-done | bytes 4194336 | tf_op jit(solution)/shard_map/ppermute | solution.py:20
  523.7 83.1 %collective-permute-done.7.refs_2_ = bf16[256,1024]{1,0:T(8,128)(2,1)} collective-permute-done((bf16[256,1024]{1,0:T(8,128)(2,1)}, bf16[256,1024]{1,0:T(8,128)(2,1)}, u32[]{:S(2)}, u32[]{:S(2)}) %collective-permute-start.7) | collective-permute-done | bytes 524320 | tf_op jit(solution)/shard_map/ppermute | solution.py:20
  621.2 38.3 %fusion.119 = (f32[1024]{0:T(1024)}, bf16[1024,4096]{0,1:T(8,128)(2,1)}, f32[1024,4096]{0,1:T(8,128)}) fusion(f32[1024]{0:T(1024)S(1)} %bitcast.454, f32[1024,4096]{0,1:T(8,128)} %copy.68, bf16[1024,1024]{1,0:T(8,128)(2,1)S(1)} %copy-done.55, f32[1024,4096]{0,1:T(8,128)} %fusion.20, f32[1024,4096]{0,1:T(8,128)} %fusion.19, f32[1024,4096]{0,1:T(8,128)} %fusion.15, ...), kind=kOutput, calls=%fused_computation.261 | convolution fusion | flops 4328520704 | bytes 114302976 | tf_op jit(solution)/shard_map/dot_general | solution.py:32
  694.3 26.1 %fusion = bf16[2048,4096]{1,0:T(8,128)(2,1)} fusion(bf16[2048,4096]{1,0:T(8,128)(2,1)} %shard_map.50, bf16[2048,1024]{1,0:T(8,128)(2,1)} %shard_map.51, bf16[1024,4096]{0,1:T(8,128)(2,1)} %get-tuple-element.75), kind=kOutput, calls=%fused_computation.8 | convolution fusion | flops 17205035008 | bytes 46137344 | tf_op jit(solution)/shard_map/dot_general | solution.py:36
  844.1 28.8 %collective-permute-done.48 = f32[2,256,1024]{2,1,0:T(8,128)} collective-permute-done((f32[2,256,1024]{2,1,0:T(8,128)}, f32[2,256,1024]{2,1,0:T(8,128)}, u32[]{:S(2)}, u32[]{:S(2)}) %collective-permute-start.48) | collective-permute-done | bytes 2097184 | tf_op jit(solution)/shard_map/ppermute | solution.py:24
  932.6 32.0 %fusion.118 = (f32[1024]{0:T(1024)}, bf16[1024,4096]{0,1:T(8,128)(2,1)}, f32[1024,4096]{0,1:T(8,128)}) fusion(f32[1024]{0:T(1024)S(1)} %bitcast.501, f32[1024,4096]{0,1:T(8,128)} %get-tuple-element.96, f32[1024,4096]{0,1:T(8,128)} %fusion.128, bf16[2048,1024]{1,0:T(8,128)(2,1)S(1)} %copy-done.56, bf16[2048,4096]{1,0:T(8,128)(2,1)} %fusion), kind=kOutput, calls=%fused_computation.260 | convolution fusion | flops 17200840704 | bytes 79699968 | tf_op jit(solution)/shard_map/dot_general | solution.py:32
  970.1 26.5 %fusion.1 = bf16[2048,4096]{1,0:T(8,128)(2,1)} fusion(bf16[2048,4096]{1,0:T(8,128)(2,1)} %shard_map.50, bf16[2048,1024]{1,0:T(8,128)(2,1)} %shard_map.54, bf16[1024,4096]{0,1:T(8,128)(2,1)} %get-tuple-element.73), kind=kOutput, calls=%fused_computation.9 | convolution fusion | flops 17205035008 | bytes 46137344 | tf_op jit(solution)/shard_map/dot_general | solution.py:36
  1029.6 26.2 %fusion.5 = bf16[2048,4096]{1,0:T(8,128)(2,1)} fusion(bf16[2048,4096]{1,0:T(8,128)(2,1)} %shard_map.56, bf16[2048,1024]{1,0:T(8,128)(2,1)} %shard_map.58, bf16[1024,4096]{0,1:T(8,128)(2,1)} %get-tuple-element.73), kind=kOutput, calls=%fused_computation.13 | convolution fusion | flops 17205035008 | bytes 46137344 | tf_op jit(solution)/shard_map/dot_general | solution.py:36
  1116.9 29.5 %collective-permute-done.71 = f32[2,256,1024]{2,1,0:T(8,128)} collective-permute-done((f32[2,256,1024]{2,1,0:T(8,128)}, f32[2,256,1024]{2,1,0:T(8,128)}, u32[]{:S(2)}, u32[]{:S(2)}) %collective-permute-start.71) | collective-permute-done | bytes 2097184 | tf_op jit(solution)/shard_map/ppermute | solution.py:24
  1201.8 32.4 %fusion.117 = (f32[1024]{0:T(1024)}, bf16[1024,4096]{0,1:T(8,128)(2,1)}, f32[1024,4096]{0,1:T(8,128)}) fusion(f32[1024]{0:T(1024)S(1)} %bitcast.502, f32[1024,4096]{0,1:T(8,128)} %get-tuple-element.97, f32[1024,4096]{0,1:T(8,128)} %fusion.131, bf16[2048,1024]{1,0:T(8,128)(2,1)S(1)} %copy-done.57, bf16[2048,4096]{1,0:T(8,128)(2,1)} %fusion.1), kind=kOutput, calls=%fused_computation.259 | convolution fusion | flops 17200840704 | bytes 79699968 | tf_op jit(solution)/shard_map/dot_general | solution.py:32
  1240.2 26.1 %fusion.2 = bf16[2048,4096]{1,0:T(8,128)(2,1)} fusion(bf16[2048,4096]{1,0:T(8,128)(2,1)} %shard_map.50, bf16[2048,1024]{1,0:T(8,128)(2,1)} %shard_map.57, bf16[1024,4096]{0,1:T(8,128)(2,1)} %get-tuple-element.71), kind=kOutput, calls=%fused_computation.10 | convolution fusion | flops 17205035008 | bytes 46137344 | tf_op jit(solution)/shard_map/dot_general | solution.py:36
  1386.3 29.5 %collective-permute-done.94 = f32[2,256,1024]{2,1,0:T(8,128)} collective-permute-done((f32[2,256,1024]{2,1,0:T(8,128)}, f32[2,256,1024]{2,1,0:T(8,128)}, u32[]{:S(2)}, u32[]{:S(2)}) %collective-permute-start.94) | collective-permute-done | bytes 2097184 | tf_op jit(solution)/shard_map/ppermute | solution.py:24
  1471.6 32.0 %fusion.116 = (f32[1024]{0:T(1024)}, bf16[1024,4096]{0,1:T(8,128)(2,1)}, f32[1024,4096]{0,1:T(8,128)}) fusion(f32[1024]{0:T(1024)S(1)} %bitcast.503, f32[1024,4096]{0,1:T(8,128)} %get-tuple-element.98, f32[1024,4096]{0,1:T(8,128)} %fusion.134, bf16[2048,1024]{1,0:T(8,128)(2,1)S(1)} %copy-done.58, bf16[2048,4096]{1,0:T(8,128)(2,1)} %fusion.2), kind=kOutput, calls=%fused_computation.258 | convolution fusion | flops 17200840704 | bytes 79699968 | tf_op jit(solution)/shard_map/dot_general | solution.py:32
  1509.1 26.2 %fusion.3 = bf16[2048,4096]{1,0:T(8,128)(2,1)} fusion(bf16[2048,4096]{1,0:T(8,128)(2,1)} %shard_map.50, bf16[2048,1024]{1,0:T(8,128)(2,1)} %shard_map.59, bf16[1024,4096]{0,1:T(8,128)(2,1)} %get-tuple-element.69), kind=kOutput, calls=%fused_computation.11 | convolution fusion | flops 17205035008 | bytes 46137344 | tf_op jit(solution)/shard_map/dot_general | solution.py:36
  1568.4 26.2 %fusion.7 = bf16[2048,4096]{1,0:T(8,128)(2,1)} fusion(bf16[2048,4096]{1,0:T(8,128)(2,1)} %shard_map.56, bf16[2048,1024]{1,0:T(8,128)(2,1)} %shard_map.62, bf16[1024,4096]{0,1:T(8,128)(2,1)} %get-tuple-element.69), kind=kOutput, calls=%fused_computation.15 | convolution fusion | flops 17205035008 | bytes 46137344 | tf_op jit(solution)/shard_map/dot_general | solution.py:36
  1673.3 28.1 %collective-permute-done.117 = f32[2,256,1024]{2,1,0:T(8,128)S(1)} collective-permute-done((f32[2,256,1024]{2,1,0:T(8,128)S(1)}, f32[2,256,1024]{2,1,0:T(8,128)S(1)}, u32[]{:S(2)}, u32[]{:S(2)}) %collective-permute-start.117) | collective-permute-done | bytes 2097184 | tf_op jit(solution)/shard_map/ppermute | solution.py:24
  1704.5 34.1 %fusion.115 = (bf16[1024,4096]{0,1:T(8,128)(2,1)}, f32[1024]{0:T(1024)S(1)}, f32[1024,4096]{0,1:T(8,128)}) fusion(f32[1024]{0:T(1024)S(1)} %bitcast.504, f32[1024,4096]{0,1:T(8,128)} %get-tuple-element.99, f32[1024,4096]{0,1:T(8,128)} %fusion.137, bf16[2048,1024]{1,0:T(8,128)(2,1)} %shard_map.59, bf16[2048,4096]{1,0:T(8,128)(2,1)} %fusion.3), kind=kOutput, calls=%fused_computation.257 | convolution fusion | flops 17200840704 | bytes 79699968 | tf_op jit(solution)/shard_map/dot_general | solution.py:32
  2040.5 32.6 %collective-permute-done.114 = f32[2,256,1024]{2,1,0:T(8,128)} collective-permute-done((f32[2,256,1024]{2,1,0:T(8,128)}, f32[2,256,1024]{2,1,0:T(8,128)}, u32[]{:S(2)}, u32[]{:S(2)}) %collective-permute-start.114) | collective-permute-done | bytes 2097184 | tf_op jit(solution)/shard_map/ppermute | solution.py:20
  2076.5 39.9 %collective-permute-done.130 = f32[2,256,1024]{2,1,0:T(8,128)S(1)} collective-permute-done((f32[2,256,1024]{2,1,0:T(8,128)S(1)}, f32[2,256,1024]{2,1,0:T(8,128)S(1)}, u32[]{:S(2)}, u32[]{:S(2)}) %collective-permute-start.130) | collective-permute-done | bytes 2097184 | tf_op jit(solution)/shard_map/ppermute | solution.py:20
  2142.4 150.3 %collective-permute-done.115 = f32[256,1024]{1,0:T(8,128)} collective-permute-done((f32[256,1024]{1,0:T(8,128)}, f32[256,1024]{1,0:T(8,128)}, u32[]{:S(2)}, u32[]{:S(2)}) %collective-permute-start.115) | collective-permute-done | bytes 1048608 | tf_op jit(solution)/shard_map/ppermute | solution.py:20
  (780 shorter events, 1431.4 us)
Async XLA Ops:
  13.2 207.7 %collective-permute-start.2 = (f32[1,1024]{1,0:T(1,128)}, f32[1,1024]{1,0:T(1,128)}, u32[]{:S(2)}, u32[]{:S(2)}) collective-permute-start(f32[1,1024]{1,0:T(1,128)} %bitcast.8), channel_id=1, source_target_pairs={{0,1},{1,0},{2,3},{3,2},{4,5},{5,4},{6,7},{7,6}} | collective-permute-start | bytes 12296 | tf_op jit(solution)/shard_map/ppermute | solution.py:20
  18.5 213.5 %collective-permute-start.23 = (f32[1,1024]{1,0:T(1,128)}, f32[1,1024]{1,0:T(1,128)}, u32[]{:S(2)}, u32[]{:S(2)}) collective-permute-start(f32[1,1024]{1,0:T(1,128)} %bitcast.12), channel_id=1, source_target_pairs={{0,4},{1,5},{2,6},{3,7},{4,0},{5,1},{6,2},{7,3}} | collective-permute-start | bytes 12296 | tf_op jit(solution)/shard_map/ppermute | solution.py:20
  23.7 182.9 %collective-permute-start.17 = (bf16[256,1024]{1,0:T(8,128)(2,1)}, bf16[256,1024]{1,0:T(8,128)(2,1)}, u32[]{:S(2)}, u32[]{:S(2)}) collective-permute-start(bf16[256,1024]{1,0:T(8,128)(2,1)} %get-tuple-element.83), channel_id=1, source_target_pairs={{0,4},{1,5},{2,6},{3,7},{4,0},{5,1},{6,2},{7,3}} | collective-permute-start | bytes 1572872 | tf_op jit(solution)/shard_map/ppermute | solution.py:20
  23.7 184.3 %collective-permute-start.13 = (bf16[256,1024]{1,0:T(8,128)(2,1)}, bf16[256,1024]{1,0:T(8,128)(2,1)}, u32[]{:S(2)}, u32[]{:S(2)}) collective-permute-start(bf16[256,1024]{1,0:T(8,128)(2,1)} %get-tuple-element.82), channel_id=1, source_target_pairs={{0,4},{1,5},{2,6},{3,7},{4,0},{5,1},{6,2},{7,3}} | collective-permute-start | bytes 1572872 | tf_op jit(solution)/shard_map/ppermute | solution.py:20
  232.1 93.8 %collective-permute-start.5 = (bf16[512,4096]{1,0:T(8,128)(2,1)}, bf16[512,4096]{1,0:T(8,128)(2,1)}, u32[]{:S(2)}, u32[]{:S(2)}) collective-permute-start(bf16[512,4096]{1,0:T(8,128)(2,1)} %get-tuple-element.64), channel_id=1, source_target_pairs={{0,4},{1,5},{2,6},{3,7},{4,0},{5,1},{6,2},{7,3}} | collective-permute-start | bytes 12582920 | tf_op jit(solution)/shard_map/ppermute | solution.py:20
  259.1 156.7 %collective-permute-start.4 = (bf16[512,4096]{1,0:T(8,128)(2,1)}, bf16[512,4096]{1,0:T(8,128)(2,1)}, u32[]{:S(2)}, u32[]{:S(2)}) collective-permute-start(bf16[512,4096]{1,0:T(8,128)(2,1)} %get-tuple-element.65), channel_id=1, source_target_pairs={{0,4},{1,5},{2,6},{3,7},{4,0},{5,1},{6,2},{7,3}} | collective-permute-start | bytes 12582920 | tf_op jit(solution)/shard_map/ppermute | solution.py:20
  263.5 242.1 %collective-permute-start.21 = (bf16[512,4096]{1,0:T(8,128)(2,1)}, bf16[512,4096]{1,0:T(8,128)(2,1)}, u32[]{:S(2)}, u32[]{:S(2)}) collective-permute-start(bf16[512,4096]{1,0:T(8,128)(2,1)} %get-tuple-element.63), channel_id=1, source_target_pairs={{0,4},{1,5},{2,6},{3,7},{4,0},{5,1},{6,2},{7,3}} | collective-permute-start | bytes 12582920 | tf_op jit(solution)/shard_map/ppermute | solution.py:20
  264.3 343.5 %collective-permute-start.22 = (bf16[512,4096]{1,0:T(8,128)(2,1)}, bf16[512,4096]{1,0:T(8,128)(2,1)}, u32[]{:S(2)}, u32[]{:S(2)}) collective-permute-start(bf16[512,4096]{1,0:T(8,128)(2,1)} %get-tuple-element.62), channel_id=1, source_target_pairs={{0,4},{1,5},{2,6},{3,7},{4,0},{5,1},{6,2},{7,3}} | collective-permute-start | bytes 12582920 | tf_op jit(solution)/shard_map/ppermute | solution.py:20
  276.4 157.2 %collective-permute-start.1 = (f32[2,256,1024]{2,1,0:T(8,128)}, f32[2,256,1024]{2,1,0:T(8,128)S(1)}, u32[]{:S(2)}, u32[]{:S(2)}) collective-permute-start(f32[2,256,1024]{2,1,0:T(8,128)} %dynamic-slice_bitcast_fusion.10), channel_id=1, source_target_pairs={{0,2},{1,3},{2,0},{3,1},{4,6},{5,7},{6,4},{7,5}} | collective-permute-start | bytes 6291464 | tf_op jit(solution)/shard_map/ppermute | solution.py:20
  439.5 167.2 %collective-permute-start.7 = (bf16[256,1024]{1,0:T(8,128)(2,1)}, bf16[256,1024]{1,0:T(8,128)(2,1)}, u32[]{:S(2)}, u32[]{:S(2)}) collective-permute-start(bf16[256,1024]{1,0:T(8,128)(2,1)} %convert_element_type.200.refs_0_), channel_id=1, source_target_pairs={{0,4},{1,5},{2,6},{3,7},{4,0},{5,1},{6,2},{7,3}} | collective-permute-start | bytes 1572872 | tf_op jit(solution)/shard_map/ppermute | solution.py:20
  521.3 97.8 %collective-permute-start.6 = (bf16[256,1024]{1,0:T(8,128)(2,1)}, bf16[256,1024]{1,0:T(8,128)(2,1)}, u32[]{:S(2)}, u32[]{:S(2)}) collective-permute-start(bf16[256,1024]{1,0:T(8,128)(2,1)} %convert_element_type.200.refs_0_), channel_id=1, source_target_pairs={{0,2},{1,3},{2,0},{3,1},{4,6},{5,7},{6,4},{7,5}} | collective-permute-start | bytes 1572872 | tf_op jit(solution)/shard_map/ppermute | solution.py:20
  522.3 96.8 %collective-permute-start.9 = (bf16[256,1024]{1,0:T(8,128)(2,1)}, bf16[256,1024]{1,0:T(8,128)(2,1)S(1)}, u32[]{:S(2)}, u32[]{:S(2)}) collective-permute-start(bf16[256,1024]{1,0:T(8,128)(2,1)} %convert_element_type.200.refs_0_), channel_id=1, source_target_pairs={{0,1},{1,0},{2,3},{3,2},{4,5},{5,4},{6,7},{7,6}} | collective-permute-start | bytes 1572872 | tf_op jit(solution)/shard_map/ppermute | solution.py:20
  523.2 96.5 %collective-permute-start.38 = (bf16[256,1024]{1,0:T(8,128)(2,1)}, bf16[256,1024]{1,0:T(8,128)(2,1)S(1)}, u32[]{:S(2)}, u32[]{:S(2)}) collective-permute-start(bf16[256,1024]{1,0:T(8,128)(2,1)} %convert_element_type.214.refs_0_), channel_id=1, source_target_pairs={{0,4},{1,5},{2,6},{3,7},{4,0},{5,1},{6,2},{7,3}} | collective-permute-start | bytes 1572872 | tf_op jit(solution)/shard_map/ppermute | solution.py:20
  618.1 71.0 %collective-permute-start.37 = (bf16[256,1024]{1,0:T(8,128)(2,1)}, bf16[256,1024]{1,0:T(8,128)(2,1)S(1)}, u32[]{:S(2)}, u32[]{:S(2)}) collective-permute-start(bf16[256,1024]{1,0:T(8,128)(2,1)} %convert_element_type.214.refs_0_), channel_id=1, source_target_pairs={{0,2},{1,3},{2,0},{3,1},{4,6},{5,7},{6,4},{7,5}} | collective-permute-start | bytes 1572872 | tf_op jit(solution)/shard_map/ppermute | solution.py:20
  619.1 70.5 %collective-permute-start.11 = (bf16[256,1024]{1,0:T(8,128)(2,1)}, bf16[256,1024]{1,0:T(8,128)(2,1)}, u32[]{:S(2)}, u32[]{:S(2)}) collective-permute-start(bf16[256,1024]{1,0:T(8,128)(2,1)} %collective-permute-done.7.refs_2_), channel_id=1, source_target_pairs={{0,1},{1,0},{2,3},{3,2},{4,5},{5,4},{6,7},{7,6}} | collective-permute-start | bytes 1572872 | tf_op jit(solution)/shard_map/ppermute | solution.py:20
  619.2 70.2 %collective-permute-start.10 = (bf16[256,1024]{1,0:T(8,128)(2,1)}, bf16[256,1024]{1,0:T(8,128)(2,1)}, u32[]{:S(2)}, u32[]{:S(2)}) collective-permute-start(bf16[256,1024]{1,0:T(8,128)(2,1)} %collective-permute-done.6.refs_1_), channel_id=1, source_target_pairs={{0,1},{1,0},{2,3},{3,2},{4,5},{5,4},{6,7},{7,6}} | collective-permute-start | bytes 1572872 | tf_op jit(solution)/shard_map/ppermute | solution.py:20
  1561.7 74.9 %collective-permute-start.90 = (f32[2,2,256,1024]{3,2,1,0:T(8,128)}, f32[2,2,256,1024]{3,2,1,0:T(8,128)}, u32[]{:S(2)}, u32[]{:S(2)}) collective-permute-start(f32[2,2,256,1024]{3,2,1,0:T(8,128)} %dynamic-slice_bitcast_fusion.2), channel_id=1, source_target_pairs={{0,1},{1,0},{2,3},{3,2},{4,5},{5,4},{6,7},{7,6}} | collective-permute-start | bytes 12582920 | tf_op jit(solution)/shard_map/ppermute | solution.py:20
  1942.3 77.3 %collective-permute-start.113 = (f32[2,2,256,1024]{3,2,0,1:T(8,128)}, f32[2,2,256,1024]{3,2,0,1:T(8,128)}, u32[]{:S(2)}, u32[]{:S(2)}) collective-permute-start(f32[2,2,256,1024]{3,2,0,1:T(8,128)} %bitcast.425), channel_id=1, source_target_pairs={{0,1},{1,0},{2,3},{3,2},{4,5},{5,4},{6,7},{7,6}} | collective-permute-start | bytes 12582920 | tf_op jit(solution)/shard_map/ppermute | solution.py:20
  1996.7 371.0 %collective-permute-start.137 = (f32[1024,1024]{0,1:T(8,128)}, f32[1024,1024]{0,1:T(8,128)}, u32[]{:S(2)}, u32[]{:S(2)}) collective-permute-start(f32[1024,1024]{0,1:T(8,128)} %fusion.18), channel_id=1, source_target_pairs={{0,4},{1,5},{2,6},{3,7},{4,0},{5,1},{6,2},{7,3}} | collective-permute-start | bytes 12582920 | tf_op jit(solution)/shard_map/ppermute | solution.py:20
  2011.9 362.0 %collective-permute-start.138 = (f32[1024,1024]{0,1:T(8,128)}, f32[1024,1024]{0,1:T(8,128)}, u32[]{:S(2)}, u32[]{:S(2)}) collective-permute-start(f32[1024,1024]{0,1:T(8,128)} %fusion.17), channel_id=1, source_target_pairs={{0,4},{1,5},{2,6},{3,7},{4,0},{5,1},{6,2},{7,3}} | collective-permute-start | bytes 12582920 | tf_op jit(solution)/shard_map/ppermute | solution.py:20
  2026.9 89.5 %collective-permute-start.130 = (f32[2,256,1024]{2,1,0:T(8,128)S(1)}, f32[2,256,1024]{2,1,0:T(8,128)S(1)}, u32[]{:S(2)}, u32[]{:S(2)}) collective-permute-start(f32[2,256,1024]{2,1,0:T(8,128)S(1)} %dynamic-slice_bitcast_fusion.8), channel_id=1, source_target_pairs={{0,2},{1,3},{2,0},{3,1},{4,6},{5,7},{6,4},{7,5}} | collective-permute-start | bytes 6291464 | tf_op jit(solution)/shard_map/ppermute | solution.py:20
  2037.8 355.7 %collective-permute-start.139 = (f32[1024,1024]{0,1:T(8,128)}, f32[1024,1024]{0,1:T(8,128)}, u32[]{:S(2)}, u32[]{:S(2)}) collective-permute-start(f32[1024,1024]{0,1:T(8,128)} %fusion.16), channel_id=1, source_target_pairs={{0,4},{1,5},{2,6},{3,7},{4,0},{5,1},{6,2},{7,3}} | collective-permute-start | bytes 12582920 | tf_op jit(solution)/shard_map/ppermute | solution.py:20
  2076.2 216.5 %collective-permute-start.115 = (f32[256,1024]{1,0:T(8,128)}, f32[256,1024]{1,0:T(8,128)}, u32[]{:S(2)}, u32[]{:S(2)}) collective-permute-start(f32[256,1024]{1,0:T(8,128)} %slice_bitcast_fusion.24), channel_id=1, source_target_pairs={{0,4},{1,5},{2,6},{3,7},{4,0},{5,1},{6,2},{7,3}} | collective-permute-start | bytes 3145736 | tf_op jit(solution)/shard_map/ppermute | solution.py:20
  2117.1 198.1 %collective-permute-start.131 = (f32[256,1024]{1,0:T(8,128)S(1)}, f32[256,1024]{1,0:T(8,128)}, u32[]{:S(2)}, u32[]{:S(2)}) collective-permute-start(f32[256,1024]{1,0:T(8,128)S(1)} %slice_bitcast_fusion.22), channel_id=1, source_target_pairs={{0,4},{1,5},{2,6},{3,7},{4,0},{5,1},{6,2},{7,3}} | collective-permute-start | bytes 3145736 | tf_op jit(solution)/shard_map/ppermute | solution.py:20
  (254 other events, 5700.5 us)

commit v3 on v2

--- a/solution.py
+++ b/solution.py
@@ -5,6 +5,7 @@
 from jax import lax
 from jax.experimental import pallas as pl
 from jax.experimental.pallas import tpu as pltpu
+from jax.experimental.layout import Layout, with_layout_constraint
 from jax.sharding import PartitionSpec as P
 
 
@@ -70,40 +71,50 @@
     )(*[pieces[k] for k in keys])
 
 
-def join_kernel(side_ref, own_ref, oth0_ref, oth1_ref, out_ref):
+def join_kernel(side_ref, own_ref, oth_ref, out_ref):
     step = pl.program_id(0)
 
     @pl.when(step < 4)
     def _():
         out_ref[...] = own_ref[...]
 
-    @pl.when((step >= 4) & (step < 6))
+    @pl.when(step >= 4)
     def _():
-        out_ref[...] = oth0_ref[...]
-
-    @pl.when(step >= 6)
-    def _():
-        out_ref[...] = oth1_ref[...]
+        out_ref[...] = oth_ref[...]
+
+
+def append_kernel(all_ref, oth_ref, out_ref):
+    out_ref[...] = oth_ref[...]
 
 
 def join_rows(side, c_blk, first_row, c_oth):
     width = c_oth[0].shape[1]
     base = first_row // BLK
-    return pl.pallas_call(
+    out_shape = jax.ShapeDtypeStruct((2048, width), BF16)
+    cost = pl.CostEstimate(flops=10 ** 9, bytes_accessed=4 * 1024 * width, transcendentals=0)
+    most = pl.pallas_call(
         join_kernel,
-        out_shape=jax.ShapeDtypeStruct((2048, width), BF16),
+        out_shape=out_shape,
         grid_spec=pltpu.PrefetchScalarGridSpec(
             num_scalar_prefetch=1,
-            grid=(8,),
+            grid=(6,),
             in_specs=[
                 pl.BlockSpec((BLK, width), lambda i, s: (base + jnp.minimum(i, 3), s[0])),
-                pl.BlockSpec((BLK, width), lambda i, s: (jnp.clip(i - 4, 0, 1), 0)),
-                pl.BlockSpec((BLK, width), lambda i, s: (jnp.clip(i - 6, 0, 1), 0)),
+                pl.BlockSpec((BLK, width), lambda i, s: (jnp.maximum(i - 4, 0), 0)),
             ],
             out_specs=pl.BlockSpec((BLK, width), lambda i, s: (i, 0)),
         ),
-        cost_estimate=pl.CostEstimate(flops=10 ** 9, bytes_accessed=4 * 2048 * width, transcendentals=0),
-    )(jnp.reshape(side, (1,)).astype(jnp.int32), c_blk, *c_oth)
+        cost_estimate=cost,
+    )(jnp.reshape(side, (1,)).astype(jnp.int32), c_blk, c_oth[0])
+    return pl.pallas_call(
+        append_kernel,
+        out_shape=out_shape,
+        grid=(2,),
+        in_specs=[pl.BlockSpec(memory_space=pl.ANY), pl.BlockSpec((BLK, width), lambda i: (i, 0))],
+        out_specs=pl.BlockSpec((BLK, width), lambda i: (i + 6, 0)),
+        input_output_aliases={0: 0},
+        cost_estimate=cost,
+    )(most, c_oth[1])
 
 
 def butterfly(vec):
@@ -121,11 +132,12 @@
         mine = side * half
         theirs = (1 - side) * half
 
-        def reduce_set_x(num):
+        def reduce_set_x(num, also):
             view = num.reshape(2, 2, 2, BLK, 1024)
             tot = pick(view, core, 1) + swap(pick(view, 1 - core, 1), 1)
             tot = pick(tot, chip, 1) + swap(pick(tot, 1 - chip, 1), 2)
-            return tot[0] + swap(tot[1], 4)
+            tot, also = lax.optimization_barrier((tot, also))
+            return tot[0] + swap(tot[1], 4), also
 
         def reduce_set(num):
             view = num.reshape(2, 2, 2, BLK, 1024)
@@ -159,8 +171,7 @@
         for p in range(4):
             sent = lax.dynamic_slice(c_blk, (p * 512, theirs), (512, half))
             c_oth.append(swap(lax.optimization_barrier(sent), 4))
-        h_state = lax.dynamic_slice_in_dim(h_blk, mine, half, 1)
-        hb = h_state.astype(BF16)
+        hb = lax.dynamic_slice_in_dim(h_blk, mine, half, 1).astype(BF16)
         hb_theirs = lax.dynamic_slice_in_dim(h_blk, theirs, half, 1).astype(BF16)
         w_own = w_blk.astype(BF16)
         offset = core * 512 + chip * BLK
@@ -181,6 +192,7 @@
         q_theirs = quotient(lax.dynamic_slice_in_dim(c_blk, theirs, half, 1), w_own, hb_theirs)
         num_t = dot_nw(q_theirs, hb_theirs)
         q_own = quotient(lax.dynamic_slice_in_dim(c_blk, mine, half, 1), w_own, hb)
+        q_own = with_layout_constraint(q_own, Layout((0, 1)))
         num_w = num_t + dot_nw(q_own, hb)
         view = num_w.reshape(2, 2, 2, BLK, 1024)
         tot = pick(view, core, 1) + swap(pick(view, 1 - core, 1), 1)
@@ -188,6 +200,8 @@
         num_h = dot_nh(w_own, q_own)
         w_state = [lax.optimization_barrier(w_state[s] * num_w[s] / h_sum[None, :]) for s in range(2)]
         w_set = [gather_set(w_state[s].astype(BF16), relay=True) for s in range(2)]
+        late, _ = lax.optimization_barrier((mine, w_state[1]))
+        h_state = lax.dynamic_slice_in_dim(h_blk, late, half, 1)
         for p in range(4):
             w_part = w_oth[p // 2][(p % 2) * 512:(p % 2) * 512 + 512]
             q_oth = quotient(c_oth[p], w_part, hb)
@@ -215,24 +229,33 @@
 
         h_sum, w_sum = sums(h_part, w_state)
         h_out = jnp.zeros(h_blk.shape, F32)
+        h_fin, h_got = [], []
         num_w = [None, None]
-        for lo, hi in zip(CUTS[:-1], CUTS[1:]):
+        spans = tuple(zip(CUTS[:-1], CUTS[1:]))
+        for j, (lo, hi) in enumerate(spans):
             at = slice(lo, hi)
             q_set = [quotient(counts[s][:, at], w_set[s], hb[:, at]) for s in range(2)]
             num_h = dot_nh(w_set[0], q_set[0]) + dot_nh(w_set[1], q_set[1])
-            h_fin = h_state[:, at] * num_h / w_sum[:, None]
-            h_got = swap(h_fin, 4)
-            h_out = lax.dynamic_update_slice_in_dim(h_out, h_fin, mine + lo, 1)
-            if hi < half:
-                h_out = lax.dynamic_update_slice_in_dim(h_out, h_got, theirs + lo, 1)
+            h_fin.append(h_state[:, at] * num_h / w_sum[:, None])
+            h_got.append(swap(h_fin[j], 4))
             for s in range(2):
                 part = dot_nw(q_set[s], hb[:, at])
                 num_w[s] = part if num_w[s] is None else num_w[s] + part
+
+        def put(out, val, base, j):
+            return lax.dynamic_update_slice_in_dim(out, val, base + spans[j][0], 1)
+
+        tot, h_sum = reduce_set_x(num_w[0], h_sum)
+        w_fin = [w_state[0] * tot / h_sum[None, :]]
+        for j in range(len(spans)):
+            h_out = put(h_out, h_fin[j], mine, j)
+        num, h_out = lax.optimization_barrier((num_w[1], h_out))
+        for j in range(len(spans) - 2):
+            h_out = put(h_out, h_got[j], theirs, j)
+        tot, h_out = reduce_set_x(num, h_out)
+        w_fin.append(w_state[1] * tot / h_sum[None, :])
+        h_out = put(h_out, h_got[-2], theirs, len(spans) - 2)
         w_out = jnp.zeros(w_blk.shape, F32)
-        w_fin = []
-        for s in range(2):
-            tot = reduce_set_x(num_w[s])
-            w_fin.append(w_state[s] * tot / h_sum[None, :])
         w_fin = jnp.stack(w_fin)
         w_x = swap(w_fin, 2)
         got = [(0, 0, w_fin), (1, 0, w_x), (0, 1, swap(w_fin, 1)), (1, 1, swap(w_x, 1))]
@@ -240,8 +263,8 @@
             start = jnp.bitwise_xor(core, c) * 512 + jnp.bitwise_xor(chip, x) * BLK
             for s in range(2):
                 w_out = lax.dynamic_update_slice_in_dim(w_out, val[s], s * 1024 + start, 0)
-        w_out, h_got = lax.optimization_barrier((w_out, h_got))
-        return w_out, lax.dynamic_update_slice_in_dim(h_out, h_got, theirs + CUTS[-2], 1)
+        w_out, last = lax.optimization_barrier((w_out, h_got[-1]))
+        return w_out, put(h_out, last, theirs, len(spans) - 1)
 
 
     return jax.shard_map(

time: 2430 us -> 2490 us (1.025)
  waiting for transfers between devices: 801 us -> 890 us
  local copies, waits for them, and re-layouts: 269 us -> 229 us
    ppermute x124, waiting for transfers between devices: 627 us -> 718 us  [swap(): return lax.ppermute(val, AXES, [(i, i ^ mask) for i in range(8)])]
    unnamed x278 -> x283, local copies, waits for them, and re-layouts: 97.7 us -> 69.1 us
  transfers between devices with their start and end apart: 140 -> 140, of which waited for: 34 -> 38; matrix products, arithmetic and copies ran while one was open for 53% -> 45% of each run, Pallas kernels for 3% -> 3%
where the time goes in v3:
time: 2490 us
  matrix products  1080 us (43%)
  waiting for transfers between devices  890 us (36%)
  local copies, waits for them, and re-layouts  229 us (9%)
  other arithmetic  110 us (4%)
  starting transfers between devices  99.1 us (4%)
  Pallas kernels  76.7 us (3%)
    ppermute x124, waiting for transfers between devices, swap(): return lax.ppermute(val, AXES, [(i, i ^ mask) for i in range(8)])  718 us
    dot_general x23, matrix products, dot_nh(): lax.dot_general(w_bf, q, (((0,), (0,)), ((), ())), preferred_element_type...  398 us
    dot_general x21, matrix products, quotient(): jnp.dot(w_bf, h_bf, preferred_element_type=F32)  351 us
    dot_general x20, matrix products, dot_nw(): lax.dot_general(q, h_bf, (((1,), (1,)), ((), ())), preferred_element_type...  328 us
    ppermute x16, waiting for transfers between devices, swap_by_core(): lax.ppermute(val, AXES, [(i, i ^ (mask1 if i & 1 else mask0)) for i in ra...  172 us
    ppermute x124, starting transfers between devices, swap(): return lax.ppermute(val, AXES, [(i, i ^ mask) for i in range(8)])  81.2 us
    unnamed x283, local copies, waits for them, and re-layouts  69.1 us
  transfers between devices with their start and end apart: 140, of which 38 were waited for; matrix products, arithmetic and copies ran while one was open for 45% of the time, Pallas kernels for 3%

profile of v3, /device:TPU:0, one launch (start us, length us, event | category | flops | bytes accessed | tf_op | source)
XLA Modules:
  0.0 2485.7 jit_solution(9639190082338672537)
XLA Ops:
  25.7 27.0 %fusion.9.clone.5 = bf16[2048,4096]{1,0:T(8,128)(2,1)} fusion(bf16[2048,8192]{1,0:T(8,128)(2,1)} %own_ref.3, s32[]{:T(128)S(6)} %select_n.222, f32[1024,8192]{1,0:T(8,128)} %param.5, f32[2048,1024]{1,0:T(8,128)} %param.4), kind=kOutput, calls=%fused_computation.19.clone.clone.clone.2 | convolution fusion | flops 17207132160 | bytes 50332672 | tf_op jit(solution)/shard_map/dot_general | solution.py:37
  78.0 27.2 %fusion.8 = bf16[2048,4096]{1,0:T(8,128)(2,1)} fusion(bf16[2048,8192]{1,0:T(8,128)(2,1)} %own_ref.3, s32[]{:T(128)S(6)} %select_n.223, f32[2048,1024]{1,0:T(8,128)} %param.4, f32[1024,8192]{1,0:T(8,128)} %param.5), kind=kOutput, calls=%fused_computation.17 | convolution fusion | flops 17207132160 | bytes 50332672 | tf_op jit(solution)/shard_map/dot_general | solution.py:37
  105.2 28.6 %convolution_add_fusion = f32[2048,1024]{1,0:T(8,128)} fusion(f32[2048,1024]{1,0:T(8,128)} %fusion.22, bf16[2048,4096]{1,0:T(8,128)(2,1)} %fusion.8, f32[1024,8192]{1,0:T(8,128)} %param.5, s32[]{:T(128)S(6)} %select_n.223), kind=kOutput, calls=%fused_computation.45 | convolution fusion | flops 17181966336 | bytes 41943044 | tf_op jit(solution)/shard_map/dot_general | solution.py:29
  212.5 40.7 %collective-permute-done.4.oth_ref = bf16[512,4096]{1,0:T(8,128)(2,1)} collective-permute-done((bf16[512,4096]{1,0:T(8,128)(2,1)}, bf16[512,4096]{1,0:T(8,128)(2,1)}, u32[]{:S(2)}, u32[]{:S(2)}) %collective-permute-start.4) | collective-permute-done | bytes 4194336 | tf_op jit(solution)/shard_map/ppermute | solution.py:21
  269.8 73.3 %collective-permute-done.5.oth_ref = bf16[512,4096]{1,0:T(8,128)(2,1)} collective-permute-done((bf16[512,4096]{1,0:T(8,128)(2,1)}, bf16[512,4096]{1,0:T(8,128)(2,1)}, u32[]{:S(2)}, u32[]{:S(2)}) %collective-permute-start.5) | collective-permute-done | bytes 4194336 | tf_op jit(solution)/shard_map/ppermute | solution.py:21
  363.4 69.7 %collective-permute-done.21.oth_ref = bf16[512,4096]{1,0:T(8,128)(2,1)} collective-permute-done((bf16[512,4096]{1,0:T(8,128)(2,1)}, bf16[512,4096]{1,0:T(8,128)(2,1)}, u32[]{:S(2)}, u32[]{:S(2)}) %collective-permute-start.21) | collective-permute-done | bytes 4194336 | tf_op jit(solution)/shard_map/ppermute | solution.py:21
  456.5 66.4 %collective-permute-done.22.oth_ref = bf16[512,4096]{1,0:T(8,128)(2,1)} collective-permute-done((bf16[512,4096]{1,0:T(8,128)(2,1)}, bf16[512,4096]{1,0:T(8,128)(2,1)}, u32[]{:S(2)}, u32[]{:S(2)}) %collective-permute-start.22) | collective-permute-done | bytes 4194336 | tf_op jit(solution)/shard_map/ppermute | solution.py:21
  601.3 38.3 %fusion.117 = (f32[1024]{0:T(1024)}, bf16[1024,4096]{0,1:T(8,128)(2,1)}, f32[1024,4096]{0,1:T(8,128)}) fusion(f32[1024]{0:T(1024)S(1)} %bitcast.441, f32[1024,4096]{0,1:T(8,128)} %copy.68, bf16[1024,1024]{1,0:T(8,128)(2,1)S(1)} %copy-done.56, f32[1024,4096]{0,1:T(8,128)} %fusion.20, f32[1024,4096]{0,1:T(8,128)} %fusion.19, f32[1024,4096]{0,1:T(8,128)} %fusion.15, ...), kind=kOutput, calls=%fused_computation.259 | convolution fusion | flops 4328520704 | bytes 114302976 | tf_op jit(solution)/shard_map/dot_general | solution.py:33
  794.8 28.6 %collective-permute-done.25 = f32[2,256,1024]{2,1,0:T(8,128)} collective-permute-done((f32[2,256,1024]{2,1,0:T(8,128)}, f32[2,256,1024]{2,1,0:T(8,128)}, u32[]{:S(2)}, u32[]{:S(2)}) %collective-permute-start.25) | collective-permute-done | bytes 2097184 | tf_op jit(solution)/shard_map/ppermute | solution.py:25
  883.4 32.0 %fusion.116 = (f32[1024]{0:T(1024)}, bf16[1024,4096]{0,1:T(8,128)(2,1)}, f32[1024,4096]{0,1:T(8,128)}) fusion(f32[1024]{0:T(1024)S(1)} %bitcast.488, f32[1024,4096]{0,1:T(8,128)} %get-tuple-element.110, f32[1024,4096]{0,1:T(8,128)} %fusion.126, bf16[2048,1024]{1,0:T(8,128)(2,1)S(1)} %copy-done.57, bf16[2048,4096]{1,0:T(8,128)(2,1)} %fusion), kind=kOutput, calls=%fused_computation.258 | convolution fusion | flops 17200840704 | bytes 79699968 | tf_op jit(solution)/shard_map/dot_general | solution.py:33
  920.9 26.3 %fusion.5 = bf16[2048,4096]{1,0:T(8,128)(2,1)} fusion(bf16[2048,4096]{1,0:T(8,128)(2,1)} %shard_map.58, bf16[2048,1024]{1,0:T(8,128)(2,1)} %shard_map.60, bf16[1024,4096]{0,1:T(8,128)(2,1)} %get-tuple-element.87), kind=kOutput, calls=%fused_computation.13 | convolution fusion | flops 17205035008 | bytes 46137344 | tf_op jit(solution)/shard_map/dot_general | solution.py:37
  980.3 26.2 %fusion.1 = bf16[2048,4096]{1,0:T(8,128)(2,1)} fusion(bf16[2048,4096]{1,0:T(8,128)(2,1)} %shard_map.51, bf16[2048,1024]{1,0:T(8,128)(2,1)} %shard_map.55, bf16[1024,4096]{0,1:T(8,128)(2,1)} %get-tuple-element.87), kind=kOutput, calls=%fused_computation.9 | convolution fusion | flops 17205035008 | bytes 46137344 | tf_op jit(solution)/shard_map/dot_general | solution.py:37
  1068.5 28.7 %collective-permute-done.45 = f32[2,256,1024]{2,1,0:T(8,128)} collective-permute-done((f32[2,256,1024]{2,1,0:T(8,128)}, f32[2,256,1024]{2,1,0:T(8,128)}, u32[]{:S(2)}, u32[]{:S(2)}) %collective-permute-start.45) | collective-permute-done | bytes 2097184 | tf_op jit(solution)/shard_map/ppermute | solution.py:25
  1152.6 32.4 %fusion.115 = (f32[1024]{0:T(1024)}, bf16[1024,4096]{0,1:T(8,128)(2,1)}, f32[1024,4096]{0,1:T(8,128)}) fusion(f32[1024]{0:T(1024)S(1)} %bitcast.489, f32[1024,4096]{0,1:T(8,128)} %get-tuple-element.111, f32[1024,4096]{0,1:T(8,128)} %fusion.129, bf16[2048,1024]{1,0:T(8,128)(2,1)S(1)} %copy-done.59, bf16[2048,4096]{1,0:T(8,128)(2,1)} %fusion.1), kind=kOutput, calls=%fused_computation.257 | convolution fusion | flops 17200840704 | bytes 79699968 | tf_op jit(solution)/shard_map/dot_general | solution.py:33
  1249.6 26.1 %fusion.2 = bf16[2048,4096]{1,0:T(8,128)(2,1)} fusion(bf16[2048,4096]{1,0:T(8,128)(2,1)} %shard_map.51, bf16[2048,1024]{1,0:T(8,128)(2,1)} %shard_map.59, bf16[1024,4096]{0,1:T(8,128)(2,1)} %get-tuple-element.85), kind=kOutput, calls=%fused_computation.10 | convolution fusion | flops 17205035008 | bytes 46137344 | tf_op jit(solution)/shard_map/dot_general | solution.py:37
  1337.6 28.7 %collective-permute-done.68 = f32[2,256,1024]{2,1,0:T(8,128)} collective-permute-done((f32[2,256,1024]{2,1,0:T(8,128)}, f32[2,256,1024]{2,1,0:T(8,128)}, u32[]{:S(2)}, u32[]{:S(2)}) %collective-permute-start.68) | collective-permute-done | bytes 2097184 | tf_op jit(solution)/shard_map/ppermute | solution.py:25
  1422.2 32.0 %fusion.114 = (f32[1024]{0:T(1024)}, bf16[1024,4096]{0,1:T(8,128)(2,1)}, f32[1024,4096]{0,1:T(8,128)}) fusion(f32[1024]{0:T(1024)S(1)} %bitcast.490, f32[1024,4096]{0,1:T(8,128)} %get-tuple-element.112, f32[1024,4096]{0,1:T(8,128)} %fusion.132, bf16[2048,1024]{1,0:T(8,128)(2,1)S(1)} %copy-done.60, bf16[2048,4096]{1,0:T(8,128)(2,1)} %fusion.2), kind=kOutput, calls=%fused_computation.256 | convolution fusion | flops 17200840704 | bytes 79699968 | tf_op jit(solution)/shard_map/dot_general | solution.py:33
  1459.7 26.1 %fusion.7 = bf16[2048,4096]{1,0:T(8,128)(2,1)} fusion(bf16[2048,4096]{1,0:T(8,128)(2,1)} %shard_map.58, bf16[2048,1024]{1,0:T(8,128)(2,1)} %shard_map.64, bf16[1024,4096]{0,1:T(8,128)(2,1)} %get-tuple-element.83), kind=kOutput, calls=%fused_computation.15 | convolution fusion | flops 17205035008 | bytes 46137344 | tf_op jit(solution)/shard_map/dot_general | solution.py:37
  1518.8 26.3 %fusion.3 = bf16[2048,4096]{1,0:T(8,128)(2,1)} fusion(bf16[2048,4096]{1,0:T(8,128)(2,1)} %shard_map.51, bf16[2048,1024]{1,0:T(8,128)(2,1)} %shard_map.61, bf16[1024,4096]{0,1:T(8,128)(2,1)} %get-tuple-element.83), kind=kOutput, calls=%fused_computation.11 | convolution fusion | flops 17205035008 | bytes 46137344 | tf_op jit(solution)/shard_map/dot_general | solution.py:37
  1623.9 28.0 %collective-permute-done.91 = f32[2,256,1024]{2,1,0:T(8,128)S(1)} collective-permute-done((f32[2,256,1024]{2,1,0:T(8,128)S(1)}, f32[2,256,1024]{2,1,0:T(8,128)S(1)}, u32[]{:S(2)}, u32[]{:S(2)}) %collective-permute-start.91) | collective-permute-done | bytes 2097184 | tf_op jit(solution)/shard_map/ppermute | solution.py:25
  1655.6 33.9 %fusion.113 = (f32[1024]{0:T(1024)S(1)}, bf16[1024,4096]{0,1:T(8,128)(2,1)}, f32[1024,4096]{0,1:T(8,128)}) fusion(f32[1024]{0:T(1024)S(1)} %bitcast.491, f32[1024,4096]{0,1:T(8,128)} %get-tuple-element.113, f32[1024,4096]{0,1:T(8,128)} %fusion.135, bf16[2048,1024]{1,0:T(8,128)(2,1)} %shard_map.61, bf16[2048,4096]{1,0:T(8,128)(2,1)} %fusion.3), kind=kOutput, calls=%fused_computation.255 | convolution fusion | flops 17200840704 | bytes 79699968 | tf_op jit(solution)/shard_map/dot_general | solution.py:33
  2061.1 213.2 %collective-permute-done.131 = f32[1024,512]{0,1:T(8,128)} collective-permute-done((f32[1024,512]{0,1:T(8,128)S(1)}, f32[1024,512]{0,1:T(8,128)}, u32[]{:S(2)}, u32[]{:S(2)}) %collective-permute-start.131) | collective-permute-done | bytes 2097184 | tf_op jit(solution)/shard_map/ppermute | solution.py:21
  2354.7 44.0 %collective-permute-done.135 = f32[2,256,1024]{2,1,0:T(8,128)S(1)} collective-permute-done((f32[2,256,1024]{2,1,0:T(8,128)}, f32[2,256,1024]{2,1,0:T(8,128)S(1)}, u32[]{:S(2)}, u32[]{:S(2)}) %collective-permute-start.135) | collective-permute-done | bytes 2097184 | tf_op jit(solution)/shard_map/ppermute | solution.py:21
  2399.5 38.8 %collective-permute-done.139 = f32[1024,1024]{0,1:T(8,128)} collective-permute-done((f32[1024,1024]{0,1:T(8,128)}, f32[1024,1024]{0,1:T(8,128)}, u32[]{:S(2)}, u32[]{:S(2)}) %collective-permute-start.139) | collective-permute-done | bytes 4194336 | tf_op jit(solution)/shard_map/ppermute | solution.py:21
  (785 shorter events, 1439.7 us)
Async XLA Ops:
  13.2 129.6 %collective-permute-start.2 = (f32[1,1024]{1,0:T(1,128)}, f32[1,1024]{1,0:T(1,128)}, u32[]{:S(2)}, u32[]{:S(2)}) collective-permute-start(f32[1,1024]{1,0:T(1,128)} %bitcast.8), channel_id=1, source_target_pairs={{0,1},{1,0},{2,3},{3,2},{4,5},{5,4},{6,7},{7,6}} | collective-permute-start | bytes 12296 | tf_op jit(solution)/shard_map/ppermute | solution.py:21
  16.7 128.5 %collective-permute-start.13 = (bf16[256,1024]{1,0:T(8,128)(2,1)}, bf16[256,1024]{1,0:T(8,128)(2,1)}, u32[]{:S(2)}, u32[]{:S(2)}) collective-permute-start(bf16[256,1024]{1,0:T(8,128)(2,1)} %get-tuple-element.96), channel_id=1, source_target_pairs={{0,4},{1,5},{2,6},{3,7},{4,0},{5,1},{6,2},{7,3}} | collective-permute-start | bytes 1572872 | tf_op jit(solution)/shard_map/ppermute | solution.py:21
  19.2 126.5 %collective-permute-start.17 = (bf16[256,1024]{1,0:T(8,128)(2,1)}, bf16[256,1024]{1,0:T(8,128)(2,1)}, u32[]{:S(2)}, u32[]{:S(2)}) collective-permute-start(bf16[256,1024]{1,0:T(8,128)(2,1)} %get-tuple-element.97), channel_id=1, source_target_pairs={{0,4},{1,5},{2,6},{3,7},{4,0},{5,1},{6,2},{7,3}} | collective-permute-start | bytes 1572872 | tf_op jit(solution)/shard_map/ppermute | solution.py:21
  23.7 122.0 %collective-permute-start.23 = (f32[1,1024]{1,0:T(1,128)}, f32[1,1024]{1,0:T(1,128)}, u32[]{:S(2)}, u32[]{:S(2)}) collective-permute-start(f32[1,1024]{1,0:T(1,128)} %bitcast.13), channel_id=1, source_target_pairs={{0,4},{1,5},{2,6},{3,7},{4,0},{5,1},{6,2},{7,3}} | collective-permute-start | bytes 12296 | tf_op jit(solution)/shard_map/ppermute | solution.py:21
  142.9 61.2 %collective-permute-start = (f32[2,2,256,1024]{3,2,0,1:T(8,128)}, f32[2,2,256,1024]{3,2,0,1:T(8,128)}, u32[]{:S(2)}, u32[]{:S(2)}) collective-permute-start(f32[2,2,256,1024]{3,2,0,1:T(8,128)} %bitcast.412), channel_id=1, source_target_pairs={{0,1},{1,0},{2,3},{3,2},{4,5},{5,4},{6,7},{7,6}} | collective-permute-start | bytes 12582920 | tf_op jit(solution)/shard_map/ppermute | solution.py:21
  159.5 93.8 %collective-permute-start.4 = (bf16[512,4096]{1,0:T(8,128)(2,1)}, bf16[512,4096]{1,0:T(8,128)(2,1)}, u32[]{:S(2)}, u32[]{:S(2)}) collective-permute-start(bf16[512,4096]{1,0:T(8,128)(2,1)} %get-tuple-element.79), channel_id=1, source_target_pairs={{0,4},{1,5},{2,6},{3,7},{4,0},{5,1},{6,2},{7,3}} | collective-permute-start | bytes 12582920 | tf_op jit(solution)/shard_map/ppermute | solution.py:21
  195.4 147.8 %collective-permute-start.5 = (bf16[512,4096]{1,0:T(8,128)(2,1)}, bf16[512,4096]{1,0:T(8,128)(2,1)}, u32[]{:S(2)}, u32[]{:S(2)}) collective-permute-start(bf16[512,4096]{1,0:T(8,128)(2,1)} %get-tuple-element.78), channel_id=1, source_target_pairs={{0,4},{1,5},{2,6},{3,7},{4,0},{5,1},{6,2},{7,3}} | collective-permute-start | bytes 12582920 | tf_op jit(solution)/shard_map/ppermute | solution.py:21
  199.1 234.0 %collective-permute-start.21 = (bf16[512,4096]{1,0:T(8,128)(2,1)}, bf16[512,4096]{1,0:T(8,128)(2,1)}, u32[]{:S(2)}, u32[]{:S(2)}) collective-permute-start(bf16[512,4096]{1,0:T(8,128)(2,1)} %get-tuple-element.77), channel_id=1, source_target_pairs={{0,4},{1,5},{2,6},{3,7},{4,0},{5,1},{6,2},{7,3}} | collective-permute-start | bytes 12582920 | tf_op jit(solution)/shard_map/ppermute | solution.py:21
  200.4 322.6 %collective-permute-start.22 = (bf16[512,4096]{1,0:T(8,128)(2,1)}, bf16[512,4096]{1,0:T(8,128)(2,1)}, u32[]{:S(2)}, u32[]{:S(2)}) collective-permute-start(bf16[512,4096]{1,0:T(8,128)(2,1)} %get-tuple-element.76), channel_id=1, source_target_pairs={{0,4},{1,5},{2,6},{3,7},{4,0},{5,1},{6,2},{7,3}} | collective-permute-start | bytes 12582920 | tf_op jit(solution)/shard_map/ppermute | solution.py:21
  212.0 237.5 %collective-permute-start.1 = (f32[2,256,1024]{2,1,0:T(8,128)}, f32[2,256,1024]{2,1,0:T(8,128)}, u32[]{:S(2)}, u32[]{:S(2)}) collective-permute-start(f32[2,256,1024]{2,1,0:T(8,128)} %dynamic-slice_bitcast_fusion.10), channel_id=1, source_target_pairs={{0,2},{1,3},{2,0},{3,1},{4,6},{5,7},{6,4},{7,5}} | collective-permute-start | bytes 6291464 | tf_op jit(solution)/shard_map/ppermute | solution.py:21
  456.0 112.4 %collective-permute-start.38 = (bf16[256,1024]{1,0:T(8,128)(2,1)}, bf16[256,1024]{1,0:T(8,128)(2,1)}, u32[]{:S(2)}, u32[]{:S(2)}) collective-permute-start(bf16[256,1024]{1,0:T(8,128)(2,1)} %convert_element_type.214.refs_0_), channel_id=1, source_target_pairs={{0,4},{1,5},{2,6},{3,7},{4,0},{5,1},{6,2},{7,3}} | collective-permute-start | bytes 1572872 | tf_op jit(solution)/shard_map/ppermute | solution.py:21
  566.5 73.0 %collective-permute-start.6 = (bf16[256,1024]{1,0:T(8,128)(2,1)}, bf16[256,1024]{1,0:T(8,128)(2,1)S(1)}, u32[]{:S(2)}, u32[]{:S(2)}) collective-permute-start(bf16[256,1024]{1,0:T(8,128)(2,1)} %convert_element_type.200.refs_0_), channel_id=1, source_target_pairs={{0,2},{1,3},{2,0},{3,1},{4,6},{5,7},{6,4},{7,5}} | collective-permute-start | bytes 1572872 | tf_op jit(solution)/shard_map/ppermute | solution.py:21
  697.6 59.5 %collective-permute-start.47 = (f32[2,2,256,1024]{3,2,1,0:T(8,128)}, f32[2,2,256,1024]{3,2,1,0:T(8,128)}, u32[]{:S(2)}, u32[]{:S(2)}) collective-permute-start(f32[2,2,256,1024]{3,2,1,0:T(8,128)} %dynamic-slice_bitcast_fusion.5), channel_id=1, source_target_pairs={{0,1},{1,0},{2,3},{3,2},{4,5},{5,4},{6,7},{7,6}} | collective-permute-start | bytes 12582920 | tf_op jit(solution)/shard_map/ppermute | solution.py:21
  915.4 58.7 %collective-permute-start.33 = (bf16[256,1024]{1,0:T(8,128)(2,1)}, bf16[256,1024]{1,0:T(8,128)(2,1)S(1)}, u32[]{:S(2)}, u32[]{:S(2)}) collective-permute-start(bf16[256,1024]{1,0:T(8,128)(2,1)} %convert_element_type.213.refs_0_), channel_id=1, source_target_pairs={{0,1},{1,0},{2,3},{3,2},{4,5},{5,4},{6,7},{7,6}} | collective-permute-start | bytes 1572872 | tf_op jit(solution)/shard_map/ppermute | solution.py:21
  1512.2 74.9 %collective-permute-start.115 = (f32[2,2,256,1024]{3,2,1,0:T(8,128)}, f32[2,2,256,1024]{3,2,1,0:T(8,128)}, u32[]{:S(2)}, u32[]{:S(2)}) collective-permute-start(f32[2,2,256,1024]{3,2,1,0:T(8,128)} %dynamic-slice_bitcast_fusion), channel_id=1, source_target_pairs={{0,1},{1,0},{2,3},{3,2},{4,5},{5,4},{6,7},{7,6}} | collective-permute-start | bytes 12582920 | tf_op jit(solution)/shard_map/ppermute | solution.py:21
  1622.6 67.0 %collective-permute-start.117 = (f32[256,1024]{1,0:T(8,128)S(1)}, f32[256,1024]{1,0:T(8,128)S(1)}, u32[]{:S(2)}, u32[]{:S(2)}) collective-permute-start(f32[256,1024]{1,0:T(8,128)S(1)} %dynamic-slice_bitcast_fusion.11), channel_id=1, source_target_pairs={{0,4},{1,3},{2,6},{3,1},{4,0},{5,7},{6,2},{7,5}} | collective-permute-start | bytes 3145736 | tf_op jit(solution)/shard_map/ppermute | solution.py:25
  2046.2 231.5 %collective-permute-start.132 = (f32[1024,1024]{0,1:T(8,128)}, f32[1024,1024]{0,1:T(8,128)}, u32[]{:S(2)}, u32[]{:S(2)}) collective-permute-start(f32[1024,1024]{0,1:T(8,128)} %fusion.18), channel_id=1, source_target_pairs={{0,4},{1,5},{2,6},{3,7},{4,0},{5,1},{6,2},{7,3}} | collective-permute-start | bytes 12582920 | tf_op jit(solution)/shard_map/ppermute | solution.py:21
  2047.0 236.1 %collective-permute-start.133 = (f32[1024,1024]{0,1:T(8,128)}, f32[1024,1024]{0,1:T(8,128)}, u32[]{:S(2)}, u32[]{:S(2)}) collective-permute-start(f32[1024,1024]{0,1:T(8,128)} %fusion.17), channel_id=1, source_target_pairs={{0,4},{1,5},{2,6},{3,7},{4,0},{5,1},{6,2},{7,3}} | collective-permute-start | bytes 12582920 | tf_op jit(solution)/shard_map/ppermute | solution.py:21
  2048.3 226.1 %collective-permute-start.131 = (f32[1024,512]{0,1:T(8,128)S(1)}, f32[1024,512]{0,1:T(8,128)}, u32[]{:S(2)}, u32[]{:S(2)}) collective-permute-start(f32[1024,512]{0,1:T(8,128)S(1)} %copy-done.79), channel_id=1, source_target_pairs={{0,4},{1,5},{2,6},{3,7},{4,0},{5,1},{6,2},{7,3}} | collective-permute-start | bytes 6291464 | tf_op jit(solution)/shard_map/ppermute | solution.py:21
  2053.8 242.3 %collective-permute-start.114 = (f32[2,256,1024]{2,1,0:T(8,128)}, f32[2,256,1024]{2,1,0:T(8,128)}, u32[]{:S(2)}, u32[]{:S(2)}) collective-permute-start(f32[2,256,1024]{2,1,0:T(8,128)} %dynamic-slice_bitcast_fusion.9), channel_id=1, source_target_pairs={{0,2},{1,3},{2,0},{3,1},{4,6},{5,7},{6,4},{7,5}} | collective-permute-start | bytes 6291464 | tf_op jit(solution)/shard_map/ppermute | solution.py:21
  2060.1 240.4 %collective-permute-start.130 = (f32[2,256,1024]{2,1,0:T(8,128)}, f32[2,256,1024]{2,1,0:T(8,128)}, u32[]{:S(2)}, u32[]{:S(2)}) collective-permute-start(f32[2,256,1024]{2,1,0:T(8,128)} %dynamic-slice_bitcast_fusion.8), channel_id=1, source_target_pairs={{0,2},{1,3},{2,0},{3,1},{4,6},{5,7},{6,4},{7,5}} | collective-permute-start | bytes 6291464 | tf_op jit(solution)/shard_map/ppermute | solution.py:21
  2303.9 134.3 %collective-permute-start.139 = (f32[1024,1024]{0,1:T(8,128)}, f32[1024,1024]{0,1:T(8,128)}, u32[]{:S(2)}, u32[]{:S(2)}) collective-permute-start(f32[1024,1024]{0,1:T(8,128)} %fusion.16), channel_id=1, source_target_pairs={{0,4},{1,5},{2,6},{3,7},{4,0},{5,1},{6,2},{7,3}} | collective-permute-start | bytes 12582920 | tf_op jit(solution)/shard_map/ppermute | solution.py:21
  2354.7 95.8 %collective-permute-start.136 = (f32[2,256,1024]{2,1,0:T(8,128)}, f32[2,256,1024]{2,1,0:T(8,128)}, u32[]{:S(2)}, u32[]{:S(2)}) collective-permute-start(f32[2,256,1024]{2,1,0:T(8,128)} %pad_maximum_fusion), channel_id=1, source_target_pairs={{0,1},{1,0},{2,3},{3,2},{4,5},{5,4},{6,7},{7,6}} | collective-permute-start | bytes 6291464 | tf_op jit(solution)/shard_map/ppermute | solution.py:21
  2398.7 83.1 %collective-permute-start.138 = (f32[1024,512]{0,1:T(8,128)}, f32[1024,512]{0,1:T(8,128)}, u32[]{:S(2)}, u32[]{:S(2)}) collective-permute-start(f32[1024,512]{0,1:T(8,128)} %fusion.23), channel_id=1, source_target_pairs={{0,4},{1,5},{2,6},{3,7},{4,0},{5,1},{6,2},{7,3}} | collective-permute-start | bytes 6291464 | tf_op jit(solution)/shard_map/ppermute | solution.py:21
  (257 other events, 5722.5 us)

commit v4 on v3

--- a/solution.py
+++ b/solution.py
@@ -256,13 +256,12 @@
         w_fin.append(w_state[1] * tot / h_sum[None, :])
         h_out = put(h_out, h_got[-2], theirs, len(spans) - 2)
         w_out = jnp.zeros(w_blk.shape, F32)
-        w_fin = jnp.stack(w_fin)
-        w_x = swap(w_fin, 2)
-        got = [(0, 0, w_fin), (1, 0, w_x), (0, 1, swap(w_fin, 1)), (1, 1, swap(w_x, 1))]
-        for x, c, val in got:
-            start = jnp.bitwise_xor(core, c) * 512 + jnp.bitwise_xor(chip, x) * BLK
-            for s in range(2):
-                w_out = lax.dynamic_update_slice_in_dim(w_out, val[s], s * 1024 + start, 0)
+        for s in range(2):
+            w_x = swap(w_fin[s], 2)
+            got = [(0, 0, w_fin[s]), (1, 0, w_x), (0, 1, swap(w_fin[s], 1)), (1, 1, swap(w_x, 1))]
+            for x, c, val in got:
+                at = s * 1024 + jnp.bitwise_xor(core, c) * 512 + jnp.bitwise_xor(chip, x) * BLK
+                w_out = lax.dynamic_update_slice_in_dim(w_out, val, at, 0)
         w_out, last = lax.optimization_barrier((w_out, h_got[-1]))
         return w_out, put(h_out, last, theirs, len(spans) - 1)
 

time: 2490 us -> 2480 us (level)
    ppermute x124 -> x127, waiting for transfers between devices: 718 us -> 710 us  [swap(): return lax.ppermute(val, AXES, [(i, i ^ mask) for i in range(8)])]
    unnamed x283 -> x271, local copies, waits for them, and re-layouts: 69.1 us -> 65.3 us
    ppermute x124 -> x127, starting transfers between devices: 81.2 us -> 84 us  [swap(): return lax.ppermute(val, AXES, [(i, i ^ mask) for i in range(8)])]
  transfers between devices with their start and end apart: 140 -> 143, of which waited for: 38 -> 37; matrix products, arithmetic and copies ran while one was open for 45% -> 45% of each run, Pallas kernels for 3% -> 3%
where the time goes in v4:
time: 2480 us; the launch traced here: 2470 us
  matrix products  1080 us (44%)
  waiting for transfers between devices  881 us (36%)
  local copies, waits for them, and re-layouts  225 us (9%)
  other arithmetic  111 us (4%)
  starting transfers between devices  102 us (4%)
  Pallas kernels  76.7 us (3%)
    ppermute x127, waiting for transfers between devices, swap(): return lax.ppermute(val, AXES, [(i, i ^ mask) for i in range(8)])  710 us
    dot_general x23, matrix products, dot_nh(): lax.dot_general(w_bf, q, (((0,), (0,)), ((), ())), preferred_element_type...  401 us
    dot_general x21, matrix products, quotient(): jnp.dot(w_bf, h_bf, preferred_element_type=F32)  351 us
    dot_general x20, matrix products, dot_nw(): lax.dot_general(q, h_bf, (((1,), (1,)), ((), ())), preferred_element_type...  324 us
    ppermute x16, waiting for transfers between devices, swap_by_core(): lax.ppermute(val, AXES, [(i, i ^ (mask1 if i & 1 else mask0)) for i in ra...  171 us
    ppermute x127, starting transfers between devices, swap(): return lax.ppermute(val, AXES, [(i, i ^ mask) for i in range(8)])  84 us
    unnamed x271, local copies, waits for them, and re-layouts  65.3 us
  transfers between devices with their start and end apart: 143, of which 37 were waited for; matrix products, arithmetic and copies ran while one was open for 45% of the time, Pallas kernels for 3%

profile of v4, /device:TPU:0, one launch (start us, length us, event | category | flops | bytes accessed | tf_op | source)
XLA Modules:
  0.0 2474.3 jit_solution(6022004058444958229)
XLA Ops:
  25.8 27.0 %fusion.9.clone.5 = bf16[2048,4096]{1,0:T(8,128)(2,1)} fusion(bf16[2048,8192]{1,0:T(8,128)(2,1)} %own_ref.3, s32[]{:T(128)S(6)} %select_n.224, f32[1024,8192]{1,0:T(8,128)} %param.5, f32[2048,1024]{1,0:T(8,128)} %param.4), kind=kOutput, calls=%fused_computation.19.clone.clone.clone.2 | convolution fusion | flops 17207132160 | bytes 50332672 | tf_op jit(solution)/shard_map/dot_general | solution.py:37
  78.0 27.2 %fusion.8 = bf16[2048,4096]{1,0:T(8,128)(2,1)} fusion(bf16[2048,8192]{1,0:T(8,128)(2,1)} %own_ref.3, s32[]{:T(128)S(6)} %select_n.225, f32[2048,1024]{1,0:T(8,128)} %param.4, f32[1024,8192]{1,0:T(8,128)} %param.5), kind=kOutput, calls=%fused_computation.17 | convolution fusion | flops 17207132160 | bytes 50332672 | tf_op jit(solution)/shard_map/dot_general | solution.py:37
  105.2 28.6 %convolution_add_fusion = f32[2048,1024]{1,0:T(8,128)} fusion(f32[2048,1024]{1,0:T(8,128)} %fusion.22, bf16[2048,4096]{1,0:T(8,128)(2,1)} %fusion.8, f32[1024,8192]{1,0:T(8,128)} %param.5, s32[]{:T(128)S(6)} %select_n.225), kind=kOutput, calls=%fused_computation.45 | convolution fusion | flops 17181966336 | bytes 41943044 | tf_op jit(solution)/shard_map/dot_general | solution.py:29
  212.6 40.7 %collective-permute-done.4.oth_ref = bf16[512,4096]{1,0:T(8,128)(2,1)} collective-permute-done((bf16[512,4096]{1,0:T(8,128)(2,1)}, bf16[512,4096]{1,0:T(8,128)(2,1)}, u32[]{:S(2)}, u32[]{:S(2)}) %collective-permute-start.4) | collective-permute-done | bytes 4194336 | tf_op jit(solution)/shard_map/ppermute | solution.py:21
  269.9 73.3 %collective-permute-done.5.oth_ref = bf16[512,4096]{1,0:T(8,128)(2,1)} collective-permute-done((bf16[512,4096]{1,0:T(8,128)(2,1)}, bf16[512,4096]{1,0:T(8,128)(2,1)}, u32[]{:S(2)}, u32[]{:S(2)}) %collective-permute-start.5) | collective-permute-done | bytes 4194336 | tf_op jit(solution)/shard_map/ppermute | solution.py:21
  363.3 69.7 %collective-permute-done.21.oth_ref = bf16[512,4096]{1,0:T(8,128)(2,1)} collective-permute-done((bf16[512,4096]{1,0:T(8,128)(2,1)}, bf16[512,4096]{1,0:T(8,128)(2,1)}, u32[]{:S(2)}, u32[]{:S(2)}) %collective-permute-start.21) | collective-permute-done | bytes 4194336 | tf_op jit(solution)/shard_map/ppermute | solution.py:21
  456.5 66.5 %collective-permute-done.22.oth_ref = bf16[512,4096]{1,0:T(8,128)(2,1)} collective-permute-done((bf16[512,4096]{1,0:T(8,128)(2,1)}, bf16[512,4096]{1,0:T(8,128)(2,1)}, u32[]{:S(2)}, u32[]{:S(2)}) %collective-permute-start.22) | collective-permute-done | bytes 4194336 | tf_op jit(solution)/shard_map/ppermute | solution.py:21
  601.2 38.3 %fusion.111 = (f32[1024]{0:T(1024)}, bf16[1024,4096]{0,1:T(8,128)(2,1)}, f32[1024,4096]{0,1:T(8,128)}) fusion(f32[1024]{0:T(1024)S(1)} %bitcast.413, f32[1024,4096]{0,1:T(8,128)} %copy.68, bf16[1024,1024]{1,0:T(8,128)(2,1)S(1)} %copy-done.53, f32[1024,4096]{0,1:T(8,128)} %fusion.20, f32[1024,4096]{0,1:T(8,128)} %fusion.19, f32[1024,4096]{0,1:T(8,128)} %fusion.15, ...), kind=kOutput, calls=%fused_computation.252 | convolution fusion | flops 4328520704 | bytes 114302976 | tf_op jit(solution)/shard_map/dot_general | solution.py:33
  704.2 26.0 %fusion = bf16[2048,4096]{1,0:T(8,128)(2,1)} fusion(bf16[2048,4096]{1,0:T(8,128)(2,1)} %shard_map.51, bf16[2048,1024]{1,0:T(8,128)(2,1)} %shard_map.52, bf16[1024,4096]{0,1:T(8,128)(2,1)} %get-tuple-element.89), kind=kOutput, calls=%fused_computation.8 | convolution fusion | flops 17205035008 | bytes 46137344 | tf_op jit(solution)/shard_map/dot_general | solution.py:37
  794.7 28.6 %collective-permute-done.25 = f32[2,256,1024]{2,1,0:T(8,128)} collective-permute-done((f32[2,256,1024]{2,1,0:T(8,128)}, f32[2,256,1024]{2,1,0:T(8,128)}, u32[]{:S(2)}, u32[]{:S(2)}) %collective-permute-start.25) | collective-permute-done | bytes 2097184 | tf_op jit(solution)/shard_map/ppermute | solution.py:25
  883.3 32.0 %fusion.110 = (f32[1024]{0:T(1024)}, bf16[1024,4096]{0,1:T(8,128)(2,1)}, f32[1024,4096]{0,1:T(8,128)}) fusion(f32[1024]{0:T(1024)S(1)} %bitcast.460, f32[1024,4096]{0,1:T(8,128)} %get-tuple-element.110, f32[1024,4096]{0,1:T(8,128)} %fusion.120, bf16[2048,1024]{1,0:T(8,128)(2,1)S(1)} %copy-done.54, bf16[2048,4096]{1,0:T(8,128)(2,1)} %fusion), kind=kOutput, calls=%fused_computation.251 | convolution fusion | flops 17200840704 | bytes 79699968 | tf_op jit(solution)/shard_map/dot_general | solution.py:33
  920.8 26.3 %fusion.5 = bf16[2048,4096]{1,0:T(8,128)(2,1)} fusion(bf16[2048,4096]{1,0:T(8,128)(2,1)} %shard_map.58, bf16[2048,1024]{1,0:T(8,128)(2,1)} %shard_map.60, bf16[1024,4096]{0,1:T(8,128)(2,1)} %get-tuple-element.87), kind=kOutput, calls=%fused_computation.13 | convolution fusion | flops 17205035008 | bytes 46137344 | tf_op jit(solution)/shard_map/dot_general | solution.py:37
  980.2 26.2 %fusion.1 = bf16[2048,4096]{1,0:T(8,128)(2,1)} fusion(bf16[2048,4096]{1,0:T(8,128)(2,1)} %shard_map.51, bf16[2048,1024]{1,0:T(8,128)(2,1)} %shard_map.55, bf16[1024,4096]{0,1:T(8,128)(2,1)} %get-tuple-element.87), kind=kOutput, calls=%fused_computation.9 | convolution fusion | flops 17205035008 | bytes 46137344 | tf_op jit(solution)/shard_map/dot_general | solution.py:37
  1068.5 28.7 %collective-permute-done.45 = f32[2,256,1024]{2,1,0:T(8,128)} collective-permute-done((f32[2,256,1024]{2,1,0:T(8,128)}, f32[2,256,1024]{2,1,0:T(8,128)}, u32[]{:S(2)}, u32[]{:S(2)}) %collective-permute-start.45) | collective-permute-done | bytes 2097184 | tf_op jit(solution)/shard_map/ppermute | solution.py:25
  1152.5 32.4 %fusion.109 = (f32[1024]{0:T(1024)}, bf16[1024,4096]{0,1:T(8,128)(2,1)}, f32[1024,4096]{0,1:T(8,128)}) fusion(f32[1024]{0:T(1024)S(1)} %bitcast.461, f32[1024,4096]{0,1:T(8,128)} %get-tuple-element.111, f32[1024,4096]{0,1:T(8,128)} %fusion.123, bf16[2048,1024]{1,0:T(8,128)(2,1)S(1)} %copy-done.56, bf16[2048,4096]{1,0:T(8,128)(2,1)} %fusion.1), kind=kOutput, calls=%fused_computation.250 | convolution fusion | flops 17200840704 | bytes 79699968 | tf_op jit(solution)/shard_map/dot_general | solution.py:33
  1337.6 28.7 %collective-permute-done.68 = f32[2,256,1024]{2,1,0:T(8,128)} collective-permute-done((f32[2,256,1024]{2,1,0:T(8,128)}, f32[2,256,1024]{2,1,0:T(8,128)}, u32[]{:S(2)}, u32[]{:S(2)}) %collective-permute-start.68) | collective-permute-done | bytes 2097184 | tf_op jit(solution)/shard_map/ppermute | solution.py:25
  1422.1 32.0 %fusion.108 = (f32[1024]{0:T(1024)}, bf16[1024,4096]{0,1:T(8,128)(2,1)}, f32[1024,4096]{0,1:T(8,128)}) fusion(f32[1024]{0:T(1024)S(1)} %bitcast.462, f32[1024,4096]{0,1:T(8,128)} %get-tuple-element.112, f32[1024,4096]{0,1:T(8,128)} %fusion.126, bf16[2048,1024]{1,0:T(8,128)(2,1)S(1)} %copy-done.57, bf16[2048,4096]{1,0:T(8,128)(2,1)} %fusion.2), kind=kOutput, calls=%fused_computation.249 | convolution fusion | flops 17200840704 | bytes 79699968 | tf_op jit(solution)/shard_map/dot_general | solution.py:33
  1459.6 26.1 %fusion.7 = bf16[2048,4096]{1,0:T(8,128)(2,1)} fusion(bf16[2048,4096]{1,0:T(8,128)(2,1)} %shard_map.58, bf16[2048,1024]{1,0:T(8,128)(2,1)} %shard_map.64, bf16[1024,4096]{0,1:T(8,128)(2,1)} %get-tuple-element.83), kind=kOutput, calls=%fused_computation.15 | convolution fusion | flops 17205035008 | bytes 46137344 | tf_op jit(solution)/shard_map/dot_general | solution.py:37
  1518.7 26.3 %fusion.3 = bf16[2048,4096]{1,0:T(8,128)(2,1)} fusion(bf16[2048,4096]{1,0:T(8,128)(2,1)} %shard_map.51, bf16[2048,1024]{1,0:T(8,128)(2,1)} %shard_map.61, bf16[1024,4096]{0,1:T(8,128)(2,1)} %get-tuple-element.83), kind=kOutput, calls=%fused_computation.11 | convolution fusion | flops 17205035008 | bytes 46137344 | tf_op jit(solution)/shard_map/dot_general | solution.py:37
  1623.8 27.9 %collective-permute-done.91 = f32[2,256,1024]{2,1,0:T(8,128)S(1)} collective-permute-done((f32[2,256,1024]{2,1,0:T(8,128)S(1)}, f32[2,256,1024]{2,1,0:T(8,128)S(1)}, u32[]{:S(2)}, u32[]{:S(2)}) %collective-permute-start.91) | collective-permute-done | bytes 2097184 | tf_op jit(solution)/shard_map/ppermute | solution.py:25
  1655.6 33.9 %fusion.107 = (f32[1024]{0:T(1024)S(1)}, bf16[1024,4096]{0,1:T(8,128)(2,1)}, f32[1024,4096]{0,1:T(8,128)}) fusion(f32[1024]{0:T(1024)S(1)} %bitcast.463, f32[1024,4096]{0,1:T(8,128)} %get-tuple-element.113, f32[1024,4096]{0,1:T(8,128)} %fusion.129, bf16[2048,1024]{1,0:T(8,128)(2,1)} %shard_map.61, bf16[2048,4096]{1,0:T(8,128)(2,1)} %fusion.3), kind=kOutput, calls=%fused_computation.248 | convolution fusion | flops 17200840704 | bytes 79699968 | tf_op jit(solution)/shard_map/dot_general | solution.py:33
  2053.3 42.3 %collective-permute-done.114 = f32[2,256,1024]{2,1,0:T(8,128)S(1)} collective-permute-done((f32[2,256,1024]{2,1,0:T(8,128)S(1)}, f32[2,256,1024]{2,1,0:T(8,128)S(1)}, u32[]{:S(2)}, u32[]{:S(2)}) %collective-permute-start.114) | collective-permute-done | bytes 2097184 | tf_op jit(solution)/shard_map/ppermute | solution.py:21
  2100.3 199.0 %collective-permute-done.121 = f32[256,1024]{1,0:T(8,128)S(1)} collective-permute-done((f32[256,1024]{1,0:T(8,128)S(1)}, f32[256,1024]{1,0:T(8,128)S(1)}, u32[]{:S(2)}, u32[]{:S(2)}) %collective-permute-start.121) | collective-permute-done | bytes 1048608 | tf_op jit(solution)/shard_map/ppermute | solution.py:21
  2341.3 78.8 %collective-permute-done.137 = f32[256,1024]{1,0:T(8,128)} collective-permute-done((f32[256,1024]{1,0:T(8,128)}, f32[256,1024]{1,0:T(8,128)}, u32[]{:S(2)}, u32[]{:S(2)}) %collective-permute-start.137) | collective-permute-done | bytes 1048608 | tf_op jit(solution)/shard_map/ppermute | solution.py:21
  (778 shorter events, 1404.5 us)
Async XLA Ops:
  13.2 129.6 %collective-permute-start.2 = (f32[1,1024]{1,0:T(1,128)}, f32[1,1024]{1,0:T(1,128)}, u32[]{:S(2)}, u32[]{:S(2)}) collective-permute-start(f32[1,1024]{1,0:T(1,128)} %bitcast.8), channel_id=1, source_target_pairs={{0,1},{1,0},{2,3},{3,2},{4,5},{5,4},{6,7},{7,6}} | collective-permute-start | bytes 12296 | tf_op jit(solution)/shard_map/ppermute | solution.py:21
  16.7 128.5 %collective-permute-start.13 = (bf16[256,1024]{1,0:T(8,128)(2,1)}, bf16[256,1024]{1,0:T(8,128)(2,1)}, u32[]{:S(2)}, u32[]{:S(2)}) collective-permute-start(bf16[256,1024]{1,0:T(8,128)(2,1)} %get-tuple-element.96), channel_id=1, source_target_pairs={{0,4},{1,5},{2,6},{3,7},{4,0},{5,1},{6,2},{7,3}} | collective-permute-start | bytes 1572872 | tf_op jit(solution)/shard_map/ppermute | solution.py:21
  19.2 126.5 %collective-permute-start.17 = (bf16[256,1024]{1,0:T(8,128)(2,1)}, bf16[256,1024]{1,0:T(8,128)(2,1)}, u32[]{:S(2)}, u32[]{:S(2)}) collective-permute-start(bf16[256,1024]{1,0:T(8,128)(2,1)} %get-tuple-element.97), channel_id=1, source_target_pairs={{0,4},{1,5},{2,6},{3,7},{4,0},{5,1},{6,2},{7,3}} | collective-permute-start | bytes 1572872 | tf_op jit(solution)/shard_map/ppermute | solution.py:21
  23.7 122.0 %collective-permute-start.23 = (f32[1,1024]{1,0:T(1,128)}, f32[1,1024]{1,0:T(1,128)}, u32[]{:S(2)}, u32[]{:S(2)}) collective-permute-start(f32[1,1024]{1,0:T(1,128)} %bitcast.13), channel_id=1, source_target_pairs={{0,4},{1,5},{2,6},{3,7},{4,0},{5,1},{6,2},{7,3}} | collective-permute-start | bytes 12296 | tf_op jit(solution)/shard_map/ppermute | solution.py:21
  142.9 61.2 %collective-permute-start = (f32[2,2,256,1024]{3,2,0,1:T(8,128)}, f32[2,2,256,1024]{3,2,0,1:T(8,128)}, u32[]{:S(2)}, u32[]{:S(2)}) collective-permute-start(f32[2,2,256,1024]{3,2,0,1:T(8,128)} %bitcast.386), channel_id=1, source_target_pairs={{0,1},{1,0},{2,3},{3,2},{4,5},{5,4},{6,7},{7,6}} | collective-permute-start | bytes 12582920 | tf_op jit(solution)/shard_map/ppermute | solution.py:21
  159.5 93.8 %collective-permute-start.4 = (bf16[512,4096]{1,0:T(8,128)(2,1)}, bf16[512,4096]{1,0:T(8,128)(2,1)}, u32[]{:S(2)}, u32[]{:S(2)}) collective-permute-start(bf16[512,4096]{1,0:T(8,128)(2,1)} %get-tuple-element.79), channel_id=1, source_target_pairs={{0,4},{1,5},{2,6},{3,7},{4,0},{5,1},{6,2},{7,3}} | collective-permute-start | bytes 12582920 | tf_op jit(solution)/shard_map/ppermute | solution.py:21
  195.4 147.8 %collective-permute-start.5 = (bf16[512,4096]{1,0:T(8,128)(2,1)}, bf16[512,4096]{1,0:T(8,128)(2,1)}, u32[]{:S(2)}, u32[]{:S(2)}) collective-permute-start(bf16[512,4096]{1,0:T(8,128)(2,1)} %get-tuple-element.78), channel_id=1, source_target_pairs={{0,4},{1,5},{2,6},{3,7},{4,0},{5,1},{6,2},{7,3}} | collective-permute-start | bytes 12582920 | tf_op jit(solution)/shard_map/ppermute | solution.py:21
  199.1 234.0 %collective-permute-start.21 = (bf16[512,4096]{1,0:T(8,128)(2,1)}, bf16[512,4096]{1,0:T(8,128)(2,1)}, u32[]{:S(2)}, u32[]{:S(2)}) collective-permute-start(bf16[512,4096]{1,0:T(8,128)(2,1)} %get-tuple-element.77), channel_id=1, source_target_pairs={{0,4},{1,5},{2,6},{3,7},{4,0},{5,1},{6,2},{7,3}} | collective-permute-start | bytes 12582920 | tf_op jit(solution)/shard_map/ppermute | solution.py:21
  200.4 322.5 %collective-permute-start.22 = (bf16[512,4096]{1,0:T(8,128)(2,1)}, bf16[512,4096]{1,0:T(8,128)(2,1)}, u32[]{:S(2)}, u32[]{:S(2)}) collective-permute-start(bf16[512,4096]{1,0:T(8,128)(2,1)} %get-tuple-element.76), channel_id=1, source_target_pairs={{0,4},{1,5},{2,6},{3,7},{4,0},{5,1},{6,2},{7,3}} | collective-permute-start | bytes 12582920 | tf_op jit(solution)/shard_map/ppermute | solution.py:21
  212.0 237.5 %collective-permute-start.1 = (f32[2,256,1024]{2,1,0:T(8,128)}, f32[2,256,1024]{2,1,0:T(8,128)}, u32[]{:S(2)}, u32[]{:S(2)}) collective-permute-start(f32[2,256,1024]{2,1,0:T(8,128)} %dynamic-slice_bitcast_fusion.10), channel_id=1, source_target_pairs={{0,2},{1,3},{2,0},{3,1},{4,6},{5,7},{6,4},{7,5}} | collective-permute-start | bytes 6291464 | tf_op jit(solution)/shard_map/ppermute | solution.py:21
  456.0 112.3 %collective-permute-start.38 = (bf16[256,1024]{1,0:T(8,128)(2,1)}, bf16[256,1024]{1,0:T(8,128)(2,1)}, u32[]{:S(2)}, u32[]{:S(2)}) collective-permute-start(bf16[256,1024]{1,0:T(8,128)(2,1)} %convert_element_type.214.refs_0_), channel_id=1, source_target_pairs={{0,4},{1,5},{2,6},{3,7},{4,0},{5,1},{6,2},{7,3}} | collective-permute-start | bytes 1572872 | tf_op jit(solution)/shard_map/ppermute | solution.py:21
  566.5 73.0 %collective-permute-start.6 = (bf16[256,1024]{1,0:T(8,128)(2,1)}, bf16[256,1024]{1,0:T(8,128)(2,1)S(1)}, u32[]{:S(2)}, u32[]{:S(2)}) collective-permute-start(bf16[256,1024]{1,0:T(8,128)(2,1)} %convert_element_type.200.refs_0_), channel_id=1, source_target_pairs={{0,2},{1,3},{2,0},{3,1},{4,6},{5,7},{6,4},{7,5}} | collective-permute-start | bytes 1572872 | tf_op jit(solution)/shard_map/ppermute | solution.py:21
  697.5 59.5 %collective-permute-start.47 = (f32[2,2,256,1024]{3,2,1,0:T(8,128)}, f32[2,2,256,1024]{3,2,1,0:T(8,128)}, u32[]{:S(2)}, u32[]{:S(2)}) collective-permute-start(f32[2,2,256,1024]{3,2,1,0:T(8,128)} %dynamic-slice_bitcast_fusion.5), channel_id=1, source_target_pairs={{0,1},{1,0},{2,3},{3,2},{4,5},{5,4},{6,7},{7,6}} | collective-permute-start | bytes 12582920 | tf_op jit(solution)/shard_map/ppermute | solution.py:21
  915.3 58.7 %collective-permute-start.33 = (bf16[256,1024]{1,0:T(8,128)(2,1)}, bf16[256,1024]{1,0:T(8,128)(2,1)S(1)}, u32[]{:S(2)}, u32[]{:S(2)}) collective-permute-start(bf16[256,1024]{1,0:T(8,128)(2,1)} %convert_element_type.213.refs_0_), channel_id=1, source_target_pairs={{0,1},{1,0},{2,3},{3,2},{4,5},{5,4},{6,7},{7,6}} | collective-permute-start | bytes 1572872 | tf_op jit(solution)/shard_map/ppermute | solution.py:21
  915.3 58.7 %collective-permute-start.34 = (bf16[256,1024]{1,0:T(8,128)(2,1)}, bf16[256,1024]{1,0:T(8,128)(2,1)S(1)}, u32[]{:S(2)}, u32[]{:S(2)}) collective-permute-start(bf16[256,1024]{1,0:T(8,128)(2,1)} %collective-permute-done.30.refs_1_), channel_id=1, source_target_pairs={{0,1},{1,0},{2,3},{3,2},{4,5},{5,4},{6,7},{7,6}} | collective-permute-start | bytes 1572872 | tf_op jit(solution)/shard_map/ppermute | solution.py:21
  1512.1 74.9 %collective-permute-start.115 = (f32[2,2,256,1024]{3,2,1,0:T(8,128)}, f32[2,2,256,1024]{3,2,1,0:T(8,128)}, u32[]{:S(2)}, u32[]{:S(2)}) collective-permute-start(f32[2,2,256,1024]{3,2,1,0:T(8,128)} %dynamic-slice_bitcast_fusion), channel_id=1, source_target_pairs={{0,1},{1,0},{2,3},{3,2},{4,5},{5,4},{6,7},{7,6}} | collective-permute-start | bytes 12582920 | tf_op jit(solution)/shard_map/ppermute | solution.py:21
  1622.5 67.0 %collective-permute-start.117 = (f32[256,1024]{1,0:T(8,128)S(1)}, f32[256,1024]{1,0:T(8,128)S(1)}, u32[]{:S(2)}, u32[]{:S(2)}) collective-permute-start(f32[256,1024]{1,0:T(8,128)S(1)} %dynamic-slice_bitcast_fusion.11), channel_id=1, source_target_pairs={{0,4},{1,3},{2,6},{3,1},{4,0},{5,7},{6,2},{7,5}} | collective-permute-start | bytes 3145736 | tf_op jit(solution)/shard_map/ppermute | solution.py:25
  2049.1 261.3 %collective-permute-start.135 = (f32[1024,1024]{0,1:T(8,128)}, f32[1024,1024]{0,1:T(8,128)}, u32[]{:S(2)}, u32[]{:S(2)}) collective-permute-start(f32[1024,1024]{0,1:T(8,128)} %fusion.18), channel_id=1, source_target_pairs={{0,4},{1,5},{2,6},{3,7},{4,0},{5,1},{6,2},{7,3}} | collective-permute-start | bytes 12582920 | tf_op jit(solution)/shard_map/ppermute | solution.py:21
  2050.3 265.4 %collective-permute-start.136 = (f32[1024,1024]{0,1:T(8,128)}, f32[1024,1024]{0,1:T(8,128)}, u32[]{:S(2)}, u32[]{:S(2)}) collective-permute-start(f32[1024,1024]{0,1:T(8,128)} %fusion.17), channel_id=1, source_target_pairs={{0,4},{1,5},{2,6},{3,7},{4,0},{5,1},{6,2},{7,3}} | collective-permute-start | bytes 12582920 | tf_op jit(solution)/shard_map/ppermute | solution.py:21
  2051.1 254.8 %collective-permute-start.134 = (f32[1024,512]{0,1:T(8,128)S(1)}, f32[1024,512]{0,1:T(8,128)}, u32[]{:S(2)}, u32[]{:S(2)}) collective-permute-start(f32[1024,512]{0,1:T(8,128)S(1)} %copy-done.74), channel_id=1, source_target_pairs={{0,4},{1,5},{2,6},{3,7},{4,0},{5,1},{6,2},{7,3}} | collective-permute-start | bytes 6291464 | tf_op jit(solution)/shard_map/ppermute | solution.py:21
  2096.1 203.2 %collective-permute-start.121 = (f32[256,1024]{1,0:T(8,128)S(1)}, f32[256,1024]{1,0:T(8,128)S(1)}, u32[]{:S(2)}, u32[]{:S(2)}) collective-permute-start(f32[256,1024]{1,0:T(8,128)S(1)} %slice_bitcast_fusion.19), channel_id=1, source_target_pairs={{0,4},{1,5},{2,6},{3,7},{4,0},{5,1},{6,2},{7,3}} | collective-permute-start | bytes 3145736 | tf_op jit(solution)/shard_map/ppermute | solution.py:21
  2098.6 229.9 %collective-permute-start.133 = (f32[2,256,1024]{2,1,0:T(8,128)}, f32[2,256,1024]{2,1,0:T(8,128)}, u32[]{:S(2)}, u32[]{:S(2)}) collective-permute-start(f32[2,256,1024]{2,1,0:T(8,128)} %dynamic-slice_bitcast_fusion.8), channel_id=1, source_target_pairs={{0,2},{1,3},{2,0},{3,1},{4,6},{5,7},{6,4},{7,5}} | collective-permute-start | bytes 6291464 | tf_op jit(solution)/shard_map/ppermute | solution.py:21
  2305.9 140.5 %collective-permute-start.142 = (f32[1024,1024]{0,1:T(8,128)}, f32[1024,1024]{0,1:T(8,128)}, u32[]{:S(2)}, u32[]{:S(2)}) collective-permute-start(f32[1024,1024]{0,1:T(8,128)} %fusion.16), channel_id=1, source_target_pairs={{0,4},{1,5},{2,6},{3,7},{4,0},{5,1},{6,2},{7,3}} | collective-permute-start | bytes 12582920 | tf_op jit(solution)/shard_map/ppermute | solution.py:21
  2333.3 86.7 %collective-permute-start.137 = (f32[256,1024]{1,0:T(8,128)}, f32[256,1024]{1,0:T(8,128)}, u32[]{:S(2)}, u32[]{:S(2)}) collective-permute-start(f32[256,1024]{1,0:T(8,128)} %slice_bitcast_fusion.18), channel_id=1, source_target_pairs={{0,4},{1,5},{2,6},{3,7},{4,0},{5,1},{6,2},{7,3}} | collective-permute-start | bytes 3145736 | tf_op jit(solution)/shard_map/ppermute | solution.py:21
  (254 other events, 6113.6 us)
